TPU v7x, 32 devices: a whole 2x2x4 slice. The times are simulated.
32 devices in a mesh: dp: 8 (over z, x), tensor: 4 (over y, core).
Axes of the slice: x: 2, y: 2, z: 4, core: 2. Of those that a mesh axis runs over, the one named last changes fastest.
Arguments:
- tubes: bfloat16 [16, 1568, 1536], P('dp'), may hold values from -6 to 6
- tube_order: int32 [16, 1568], P('dp'), may hold values from 0 to 1567, each once within a row
- common_master: float32 [2666880], P('dp'), as said below
- common_first: float32 [2666880], P('dp'), may hold values from -4.7683716e-06 to 4.7683716e-06
- common_second: float32 [2666880], P('dp'), may hold values from 2.3706446e-13 to 7.2031123e-13
- split_master: float32 [4, 2065920], P('tensor', 'dp'), as said below
- split_first: float32 [4, 2065920], P('tensor', 'dp'), may hold values from -4.7683716e-06 to 4.7683716e-06
- split_second: float32 [4, 2065920], P('tensor', 'dp'), may hold values from 2.3706446e-13 to 7.2031123e-13
Outputs:
- loss_mean: float32 [1], replicated
- grad_norm: float32 [1], replicated
- common_new: float32 [2666880], P('dp')
- common_first_new: float32 [2666880], P('dp')
- common_second_new: float32 [2666880], P('dp')
- common_copy: bfloat16 [2666880], P('dp')
- split_new: float32 [4, 2065920], P('tensor', 'dp')
- split_first_new: float32 [4, 2065920], P('tensor', 'dp')
- split_second_new: float32 [4, 2065920], P('tensor', 'dp')
- split_copy: bfloat16 [4, 2065920], P('tensor', 'dp')
Inputs may be any that keep to these rules, and one draw needn't show every extreme that they name: `tube_order`: each row is a permutation of the 1568 tubes; its first 157 entries are the visible tubes, the rest the masked ones. `common_master`: laid out as the first step states; padding entries are drawn as well. `split_master`: laid out as the first step states; padding entries are drawn as well.
All inputs are finite; a program needn't handle non-finite values.
Results may differ from a plain program's by a relative error of at most 0.011.
The roundings to bfloat16 on the way count: a program that leaves them out, or rounds other values in their place, can miss the bound.
Values may be sent and summed in bfloat16 or wider, within the bound.
A program may use at most 320 MiB of HBM per device.

v0:
```python
import functools
import math
from types import SimpleNamespace as Namespace

import jax
import jax.numpy as jnp
import numpy as np
from jax import lax
from jax.experimental import pallas as pl
from jax.experimental.pallas import tpu as pltpu
from jax.sharding import PartitionSpec as P

DP = "dp"
TENSOR = "tensor"
D = 768
HEAD = 64
FF = 3072
DD = 384
DFF = 1536
PATCH = 1536
TUBES = 1568
VIS = 157
STEP = 10
LANES = 128
TILE = 16
BLOCK = TILE * LANES
FRONT = 24
MESH = pl.DeviceIdType.MESH
F32 = jnp.float32
BF16 = jnp.bfloat16


def round_up(value, step):
    return -(-value // step) * step


COMMON = dict(
    embedding=(PATCH, D), embedding_bias=(D,), enc_norms=(6, D), enc_biases=(2, D), to_decoder=(D, DD), mask_token=(DD,),
    dec_norms=(6, DD), dec_biases=(2, DD), dec_qkv=(DD, 3 * DD), dec_qkv_bias=(2, DD), dec_proj=(DD, DD), pixel_head=(DD, PATCH),
    head_bias=(PATCH,))
SPLIT = dict(
    enc_qkv=(D, 576), enc_qkv_bias=(2, 192), enc_proj=(192, D), enc_up=(D, 768), enc_up_bias=(768,), enc_down=(768, D),
    dec_up=(DD, 384), dec_up_bias=(384,), dec_down=(384, DD))


def row_table(layout):
    table, at = {}, 0
    for name, shape in layout.items():
        count = math.prod(shape) // LANES
        table[name] = (at, count)
        at += count
    return Namespace(**table)


CROW = row_table(COMMON)
SROW = row_table(SPLIT)
DEC_ROW = SROW.dec_up[0]
SPLIT_ROWS = SROW.dec_down[0] + SROW.dec_down[1]
COMMON_ROWS = CROW.head_bias[0] + CROW.head_bias[1]


class Plan:
    def __init__(self, parts, share, rows_step):
        self.parts, self.share = parts, share
        self.base = [i * share // BLOCK * TILE for i in range(parts)]
        self.rows = round_up(-(-(share + BLOCK - 1) // LANES), rows_step)

    def pieces(self, first, last):
        out = []
        for i in range(self.parts):
            start = self.base[i] + (TILE if i else 0)
            stop = self.base[i + 1] if i + 1 < self.parts else self.base[i] + self.rows
            low, high = max(start, first), min(stop, last)
            if i and first <= self.base[i] < last:
                out.append(("edge", i, self.base[i] - self.base[i - 1], self.base[i], TILE))
            if low < high:
                out.append(("body", i, low - self.base[i], low, high - low))
        return out

    def owners(self, first, last):
        return sorted({i for kind, i, *_ in self.pieces(first, last)} | {i - 1 for kind, i, *_ in self.pieces(first, last) if kind == "edge"})


def align_kernel(scalars, split_in, common_in, split_out, common_out):
    def move(source, target, lanes, rows_down, skip, step):
        def part(row, step):
            lane = lax.broadcasted_iota(jnp.int32, (step, LANES), 1)
            here = source[pl.ds(FRONT - rows_down + skip + row, step), :]
            before = source[pl.ds(FRONT - 1 - rows_down + skip + row, step), :]
            value = jnp.where(lane >= lanes, pltpu.roll(here, lanes, 1), pltpu.roll(before, lanes, 1))
            target[pl.ds(pl.multiple_of(row, TILE), step), :] = value.astype(BF16)

        def body(index, _):
            part(index * step, step)
            return 0

        whole = target.shape[0] // step
        lax.fori_loop(0, whole, body, 0)
        if target.shape[0] % step:
            part(whole * step, target.shape[0] % step)

    move(split_in, split_out, scalars[0], scalars[1], 0, 256)
    move(common_in, common_out, scalars[2], scalars[3], scalars[4], 256)


def aligned(master, plan):
    tail = (plan.rows + 8) * LANES - master.shape[-1]
    return jnp.pad(master, ((0, 0),) * (master.ndim - 1) + ((FRONT * LANES, tail),)).reshape(-1, LANES)


def align(common_master, split_master, cplan, splan):
    me, t = lax.axis_index(DP), lax.axis_index(TENSOR)
    soff = me * splan.share % BLOCK
    coff = me * cplan.share % BLOCK
    quarter = cplan.rows // 4
    scalars = jnp.stack([soff % LANES, soff // LANES, coff % LANES, coff // LANES, t * quarter]).astype(jnp.int32)
    return pl.pallas_call(
        align_kernel,
        out_shape=(jax.ShapeDtypeStruct((splan.rows, LANES), BF16), jax.ShapeDtypeStruct((quarter, LANES), BF16)),
        in_specs=[pl.BlockSpec(memory_space=pltpu.SMEM), pl.BlockSpec(memory_space=pltpu.VMEM), pl.BlockSpec(memory_space=pltpu.VMEM)],
        out_specs=[pl.BlockSpec(memory_space=pltpu.VMEM)] * 2,
        name="align",
    )(scalars, aligned(split_master, splan), aligned(common_master, cplan))


OUTS = Namespace(
    embedding=(PATCH, D), to_decoder=(D, DD), dec_qkv=(DD, 3 * DD), dec_proj=(DD, DD), pixel_head=(DD, PATCH),
    enc_qkv=(2, D, 576), enc_proj=(384, D), enc_up=(D, 1536), enc_down=(1536, D), dec_up=(DD, 1536), dec_down=(1536, DD))
OUT_NAMES = tuple(vars(OUTS))
CMATS = OUT_NAMES[:5]
SMALLS = ((CROW.embedding_bias[0], 54), (CROW.mask_token[0], 27), (CROW.dec_qkv_bias[0], 6), (CROW.head_bias[0], 12))


def copy_rows(pieces, frame, wide, first, chunk=64):
    for kind, part, row, at, count in pieces:
        if kind == "edge":
            wide[pl.ds(at - first, TILE), :] = frame(part)[pl.ds(0, TILE), :].astype(F32) + frame(part - 1)[pl.ds(row, TILE), :].astype(F32)
            continue
        source, whole = frame(part), count // chunk

        def body(index, _, source=source, row=row, at=at):
            wide[pl.ds(pl.multiple_of(at - first + index * chunk, TILE), chunk), :] = source[
                pl.ds(pl.multiple_of(row + index * chunk, TILE), chunk), :
            ].astype(F32)
            return 0

        if whole:
            lax.fori_loop(0, whole, body, 0)
        for rest in range(whole * chunk, count, TILE):
            wide[pl.ds(at - first + rest, TILE), :] = source[pl.ds(row + rest, TILE), :].astype(F32)


def matrix_out(wide, start, rows, width, target, row0, col0, step=64):
    per_row = width // LANES

    def body(index, _):
        at = index * step
        for j in range(per_row):
            value = wide[pl.ds(start + j + at * per_row, step, stride=per_row), :]
            target[pl.ds(pl.multiple_of(row0 + at, TILE), step), col0 + j * LANES : col0 + (j + 1) * LANES] = value.astype(BF16)
        return 0

    lax.fori_loop(0, rows // step, body, 0)


def qkv_out(wide, start, pair_buf, target):
    step = 32
    lane = lax.broadcasted_iota(jnp.int32, (step, LANES), 1)

    def body(index, _):
        at = start + index * step * 9
        for j in range(5):
            even = wide[pl.ds(at + j, step, stride=9), :]
            low = pltpu.roll(wide[pl.ds(at + 4 + j, step, stride=9), :], 64, 1)
            if j < 4:
                high = pltpu.roll(wide[pl.ds(at + 5 + j, step, stride=9), :], 64, 1)
                odd = jnp.where(lane < 64, low, high)
            else:
                odd = low
            pair_buf[j, pl.ds(0, step, stride=2), :] = even
            pair_buf[j, pl.ds(1, step, stride=2), :] = odd
            both = pair_buf[j].astype(BF16)
            rows = pl.ds(pl.multiple_of(index * 64, 64), 64)
            if j < 4:
                target[rows, j * LANES : (j + 1) * LANES] = both
            else:
                target[rows, 512:576] = both[:, :64]
        return 0

    lax.fori_loop(0, 12, body, 0)


def floor16(value):
    return value // TILE * TILE


SCALE = HEAD ** (-0.5)


def nt(a, b):
    return lax.dot_general(a, b, (((1,), (1,)), ((), ())), preferred_element_type=F32)


def nn(a, b):
    return lax.dot_general(a, b, (((1,), (0,)), ((), ())), preferred_element_type=F32)


VP = 160
SAVED = Namespace(
    embedded=((VP, D), F32), normed_a=((VP, D), BF16), mixed=((2, VP, 576), BF16), probs=((6, VP, VP), F32), merged=((VP, 384), BF16),
    after=((VP, D), F32), normed_m=((VP, D), BF16), raised=((VP, 1536), F32), active=((VP, 1536), BF16), encoded=((VP, D), F32),
    final_low=((VP, D), BF16), lowered=((VP, DD), F32))
NSAVED = len(vars(SAVED))
SMALL_AT = []
for _, _count in SMALLS:
    SMALL_AT.append(sum(round_up(count, 8) for _, count in SMALLS[: len(SMALL_AT)]))


def norm_rows(inputs, gain, shift):
    centered = inputs - jnp.mean(inputs, axis=-1, keepdims=True)
    spread = jnp.mean(centered * centered, axis=-1, keepdims=True)
    return centered * lax.rsqrt(spread + 1e-06) * gain + shift


def unpacker(cplan, splan, common_frame, split_frame, dec_frame, stage, small_ref, bias_ref, dbias_ref, wide, pair_buf, done):
    def load(plan, frame, start, count):
        first, last = floor16(start), round_up(start + count, TILE)
        copy_rows(plan.pieces(first, last), frame, wide, first)
        return start - first

    def split(c):
        frame = functools.partial(split_frame, c)
        start, count = SROW.enc_qkv
        qkv_out(wide, load(splan, frame, start, count), pair_buf, stage.enc_qkv.at[c])
        at = load(splan, frame, *SROW.enc_qkv_bias)
        bias_ref[c, 0:8, :] = wide[pl.ds(at, 8), :]
        at = load(splan, frame, *SROW.enc_proj)
        matrix_out(wide, at, 192, D, stage.enc_proj, c * 192, 0)
        at = load(splan, frame, *SROW.enc_up)
        matrix_out(wide, at, D, 768, stage.enc_up, 0, c * 768)
        at = load(splan, frame, *SROW.enc_up_bias)
        bias_ref[c, 8:16, :] = wide[pl.ds(at, 8), :]
        at = load(splan, frame, *SROW.enc_down)
        matrix_out(wide, at, 768, D, stage.enc_down, c * 768, 0)
        if c:
            for whole in (stage.enc_qkv, stage.enc_proj, stage.enc_up, stage.enc_down):
                done(whole)

    def common(name):
        at = load(cplan, common_frame, *vars(CROW)[name])
        rows, width = vars(OUTS)[name]
        matrix_out(wide, at, rows, width, vars(stage)[name], 0, 0)
        if name != CMATS[0]:
            done(vars(stage)[name])

    def smalls():
        for small_at, (start, count) in zip(SMALL_AT, SMALLS):
            at = load(cplan, common_frame, start, count)
            small_ref[pl.ds(small_at, round_up(count, 8)), :] = wide[pl.ds(at, round_up(count, 8)), :]

    def dec():
        for slot in range(4):
            frame = functools.partial(split_frame, slot) if slot < 2 else functools.partial(dec_frame, slot - 2)
            at = load(splan, frame, DEC_ROW, SPLIT_ROWS - DEC_ROW)
            matrix_out(wide, at, DD, 384, stage.dec_up, 0, slot * 384)
            bias = at + SROW.dec_up_bias[0] - DEC_ROW
            dbias_ref[slot, :, :] = wide[pl.ds(bias, 8), :]
            matrix_out(wide, bias + 3, 384, DD, stage.dec_down, slot * 384, 0)
        done(stage.dec_up)
        done(stage.dec_down)

    return split, common, smalls, dec


def row_of(ref, at, count):
    return jnp.concatenate([ref[at + k : at + k + 1, :] for k in range(count)], axis=1)


def embed(pix, pos, stage, small_ref, saved):
    saved.embedded[...] = nn(pix[...], stage.embedding[...]) + row_of(small_ref, 0, 6) + pos[...]


def encode(stage, small_ref, bias_ref, saved, swap, while_first, while_second):
    def norm(k):
        return row_of(small_ref, 6 + 6 * k, 6)

    embedded = saved.embedded[...]
    normed = norm_rows(embedded, norm(0), norm(1)).astype(BF16)
    saved.normed_a[...] = normed
    keys = lax.broadcasted_iota(jnp.int32, (VP, VP), 1) < VIS
    outs = []
    for slot in range(2):
        flat = row_of(bias_ref.at[slot], 0, 3)
        bias = jnp.concatenate([flat[:, :192], jnp.zeros((1, 192), F32), flat[:, 192:]], axis=1)
        saved.mixed[slot] = (nn(normed, stage.enc_qkv[slot]) + bias).astype(BF16)
        for head in range(3):
            q, k, v = [saved.mixed[slot, :, 192 * n + HEAD * head : 192 * n + HEAD * (head + 1)] for n in range(3)]
            scores = jnp.where(keys, nt(q, k) * SCALE, -1e30)
            shifted = jnp.exp(scores - jnp.max(scores, axis=1, keepdims=True))
            probs = shifted / jnp.sum(shifted, axis=1, keepdims=True)
            saved.probs[slot * 3 + head] = probs
            outs.append(nn(probs.astype(BF16), v).astype(BF16))
    merged = jnp.concatenate(outs, axis=1)
    saved.merged[...] = merged
    mine, copy, other = swap(0)
    mine[...] = nn(merged, stage.enc_proj[...]).astype(BF16)
    copy.start()
    while_first()
    copy.wait_recv()
    after = embedded + (mine[...].astype(F32) + other[...].astype(F32) + row_of(small_ref, 42, 6))
    saved.after[...] = after
    normed = norm_rows(after, norm(2), norm(3)).astype(BF16)
    saved.normed_m[...] = normed
    up_bias = jnp.concatenate([row_of(bias_ref.at[slot], 8, 6) for slot in range(2)], axis=1)
    for col in range(0, 1536, 384):
        raised = nn(normed, stage.enc_up[:, col : col + 384]) + up_bias[:, col : col + 384]
        saved.raised[:, col : col + 384] = raised
        saved.active[:, col : col + 384] = (0.5 * raised * (1.0 + lax.erf(raised * math.sqrt(0.5)))).astype(BF16)
    mine, second, other = swap(1)
    mine[...] = nn(saved.active[...], stage.enc_down[...]).astype(BF16)
    second.start()
    while_second()
    second.wait_recv()
    encoded = saved.after[...] + (mine[...].astype(F32) + other[...].astype(F32) + row_of(small_ref, 48, 6))
    saved.encoded[...] = encoded
    saved.final_low[...] = norm_rows(encoded, norm(4), norm(5)).astype(BF16)
    copy.wait_send()
    second.wait_send()


def unpack_and_encode(cplan, splan, refs, ready):
    pix, pos, outs, smalls, saved, (sbuf, dbuf, cbuf, wide, pair_buf), stages, out_sem, (swaps, moved, send, recv) = refs
    t = lax.axis_index(TENSOR)
    y, c = t // 2, t % 2
    me = lax.axis_index(DP)
    fd = first_dec(splan)
    stage = Namespace(**dict(zip(OUT_NAMES, stages)))
    copies = []

    def done(whole):
        index = [ref is whole for ref in stages].index(True)
        copy = pltpu.make_async_copy(whole, outs[index], out_sem.at[index])
        copy.start()
        copies.append(copy)

    split, common, common_smalls, dec = unpacker(
        cplan, splan, lambda i: cbuf.at[i], lambda c, i: sbuf.at[c, i], lambda c, i: dbuf.at[c, i - fd],
        stage, smalls[0], smalls[1], smalls[2], wide, pair_buf, done)

    def swap(n):
        copy = pltpu.make_async_remote_copy(
            src_ref=swaps.at[n, 0], dst_ref=swaps.at[n, 1], send_sem=send.at[n], recv_sem=recv.at[n],
            device_id={DP: me, TENSOR: (1 - y) * 2 + c}, device_id_type=MESH)
        return swaps.at[n, 0], copy, swaps.at[n, 1]

    ready(0)
    common(CMATS[0])
    common_smalls()
    embed(pix, pos, stage, smalls[0], saved)
    ready(1)
    split(0)
    split(1)

    def first():
        common(CMATS[1])
        common(CMATS[2])

    def second():
        common(CMATS[3])
        common(CMATS[4])

    encode(stage, smalls[0], smalls[1], saved, swap, first, second)
    move = pltpu.make_async_remote_copy(
        src_ref=saved.final_low, dst_ref=moved, send_sem=send.at[2], recv_sem=recv.at[2],
        device_id={DP: me, TENSOR: y * 2 + (1 - c)}, device_id_type=MESH)

    @pl.when(y == c)
    def _():
        move.start()

    ready(2)
    dec()

    @pl.when(y == c)
    def _():
        saved.lowered[...] = nn(saved.final_low[...], stage.to_decoder[...])
        move.wait_send()

    @pl.when(y != c)
    def _():
        move.wait_recv()
        saved.lowered[...] = nn(moved[...], stage.to_decoder[...])

    for copy in copies:
        copy.wait()


SMALL_ROWS = sum(round_up(count, 8) for _, count in SMALLS)
GATHERED = tuple(jax.ShapeDtypeStruct(vars(OUTS)[name], BF16) for name in OUT_NAMES) + (
    jax.ShapeDtypeStruct((SMALL_ROWS, LANES), F32), jax.ShapeDtypeStruct((2, 16, LANES), F32), jax.ShapeDtypeStruct((4, 8, LANES), F32),
) + tuple(jax.ShapeDtypeStruct(*pair) for pair in vars(SAVED).values())


def first_dec(splan):
    return splan.owners(floor16(DEC_ROW), round_up(SPLIT_ROWS, TILE))[0]


def unpack_scratch(cplan, splan):
    fd = first_dec(splan)
    return [
        pltpu.VMEM((2, splan.parts, splan.rows, LANES), BF16),
        pltpu.VMEM((2, splan.parts - fd, splan.rows, LANES), BF16),
        pltpu.VMEM((cplan.parts, cplan.rows, LANES), BF16),
        pltpu.VMEM((CROW.embedding[1] + 32, LANES), F32),
        pltpu.VMEM((5, 64, LANES), F32),
    ] + [pltpu.VMEM(vars(OUTS)[name], BF16) for name in OUT_NAMES] + [
        pltpu.SemaphoreType.DMA((len(OUT_NAMES),)), pltpu.VMEM((2, 2, VP, D), BF16), pltpu.VMEM((VP, D), BF16),
        pltpu.SemaphoreType.DMA((3,)), pltpu.SemaphoreType.DMA((3,))]


def shared_refs(refs):
    nout = len(OUT_NAMES)
    pix, pos = refs[:2]
    outs, smalls = refs[2 : nout + 2], refs[nout + 2 : nout + 5]
    saved = Namespace(**dict(zip(vars(SAVED), refs[nout + 5 : nout + 5 + NSAVED])))
    refs = refs[nout + 5 + NSAVED :]
    return (pix, pos, outs, smalls, saved, refs[:5], refs[5 : 5 + nout], refs[5 + nout], refs[6 + nout : 10 + nout]), refs[10 + nout :]


def gather_kernel(cplan, splan, s_own, c_own, *refs):
    shared, (send, recv, local) = shared_refs(refs)
    sbuf, dbuf, cbuf = shared[5][:3]
    me, t = lax.axis_index(DP), lax.axis_index(TENSOR)
    z, x, y, c = me // 2, me % 2, t // 2, t % 2
    ty = (1 - y) * 2 + c
    fd = first_dec(splan)
    quarter = cplan.rows // 4

    def cblock(i, tt):
        return cbuf.at[i, pl.ds(pl.multiple_of(tt * quarter, TILE), quarter)]

    def sblock(i):
        return sbuf.at[c, i]

    zdev = [{DP: (z + k) % 4 * 2 + x, TENSOR: t} for k in range(4)]
    xdev, ydev, kdev = {DP: z * 2 + (1 - x), TENSOR: t}, {DP: me, TENSOR: ty}, {DP: me, TENSOR: y * 2 + (1 - c)}
    barrier = pltpu.get_barrier_semaphore()
    for device in zdev[1:] + [xdev, ydev, kdev]:
        pl.semaphore_signal(barrier, inc=1, device_id=device, device_id_type=MESH)
    own = [pltpu.make_async_copy(s_own, sblock(me), local.at[0]), pltpu.make_async_copy(c_own, cblock(me, t), local.at[1])]
    for copy in own:
        copy.start()
    pl.semaphore_wait(barrier, 6)
    for copy in own:
        copy.wait()

    def remote(source, target, slot, device):
        return pltpu.make_async_remote_copy(
            src_ref=source, dst_ref=target, send_sem=send.at[slot], recv_sem=recv.at[slot], device_id=device, device_id_type=MESH)

    def z_copy(common, down, hop, i):
        block = cblock(i, t) if common else sblock(i)
        return remote(block, block, common * 6 + down * 3 + hop - 1, zdev[3 if down else 1])

    def x_copy(common, i):
        block = cblock(i, t) if common else sblock(i)
        return remote(block, block, 12 + common * 4 + i // 2, xdev)

    def y_copy(i):
        return remote(cblock(i, t), cblock(i, t), 20 + i, ydev)

    def k_copy(i):
        return remote(sblock(i), sblock(i), 28 + i, kdev)

    def k_common(i):
        return remote(cblock(i, t), cblock(i, t), 36 + i, kdev)

    def k_far(i):
        return remote(cblock(i, ty), cblock(i, ty), 44 + i, kdev)

    def dec_rows(i):
        return pl.ds(max(0, DEC_FIRST - splan.base[i]), min(splan.rows, S_WIDE - splan.base[i]) - max(0, DEC_FIRST - splan.base[i]))

    def d_copy(i):
        return remote(sbuf.at[c, i, dec_rows(i)], dbuf.at[c, i - fd, dec_rows(i)], 52 + i - fd, ydev)

    def d_beside(i):
        return remote(dbuf.at[c, i - fd, dec_rows(i)], dbuf.at[c, i - fd, dec_rows(i)], 54 + i - fd, kdev)

    def send_z(common, down, hop):
        i = (z + (hop - 1 if down else 1 - hop)) * 2 + x
        able = jnp.logical_and(z > 0, z + hop - 1 <= 3) if down else jnp.logical_and(z < 3, z - hop + 1 >= 0)
        return i, able

    def pass_on(common, down, hop, action):
        i, able = send_z(common, down, hop)

        @pl.when(able)
        def _():
            action(z_copy(common, down, hop, i))

    def share_c(i):
        x_copy(1, i).start()
        y_copy(i).start()
        k_common(i).start()

    def share_s(i):
        x_copy(0, i).start()
        k_copy(i).start()
        dec_start(i)

    def dec_start(i):
        for known in range(fd, splan.parts):
            @pl.when(i == known)
            def _(known=known):
                d_copy(known).start()

    for common in (1, 0):
        for down in (0, 1):
            pass_on(common, down, 1, lambda copy: copy.start())
    share_c(me)
    share_s(me)
    for hop in (1, 2, 3):
        for common in (1, 0):
            for down in (0, 1):
                i = (z + (hop if down else -hop)) * 2 + x
                here = z + hop <= 3 if down else z >= hop

                @pl.when(here)
                def _(common=common, down=down, hop=hop, i=i):
                    z_copy(common, down, hop, i).wait_recv()
                    if hop < 3:
                        pass_on(common, down, hop + 1, lambda copy: copy.start())
                    if common:
                        share_c(i)
                    else:
                        share_s(i)

    def split_here(zz):
        i = zz * 2 + (1 - x)
        x_copy(0, i).wait_recv()
        k_copy(i).start()
        dec_start(i)

    def ready(stage):
        if stage == 0:
            for zz in range(4):
                i = zz * 2 + (1 - x)
                x_copy(1, i).wait_recv()
                y_copy(i).start()
                k_common(i).start()
            for i in range(8):
                y_copy(i).wait_recv()
                k_far(i).start()
            for i in range(8):
                k_common(i).wait_recv()
                k_far(i).wait_recv()
        if stage == 1:
            for zz in range(4):
                split_here(zz)
            for i in range(8):
                k_copy(i).wait_recv()
        if stage == 2:
            for i in range(fd, splan.parts):
                d_copy(i).wait_recv()
                d_beside(i).start()
            for i in range(fd, splan.parts):
                d_beside(i).wait_recv()

    unpack_and_encode(cplan, splan, shared, ready)
    for hop in (1, 2, 3):
        for common in (1, 0):
            for down in (0, 1):
                pass_on(common, down, hop, lambda copy: copy.wait_send())
    for zz in range(4):
        for common in (1, 0):
            x_copy(common, zz * 2 + x).wait_send()
    for i in range(8):
        for copy in (y_copy(i), k_copy(i), k_common(i), k_far(i)):
            copy.wait_send()
    for i in range(fd, splan.parts):
        d_copy(i).wait_send()
        d_beside(i).wait_send()


def local_unpack_kernel(cplan, splan, s_all, d_all, c_all, *refs):
    shared, (local,) = shared_refs(refs)
    t = lax.axis_index(TENSOR)
    barrier = pltpu.get_barrier_semaphore()
    for other in (t // 2 * 2 + 1 - t % 2, (1 - t // 2) * 2 + t % 2):
        pl.semaphore_signal(barrier, inc=1, device_id={DP: lax.axis_index(DP), TENSOR: other}, device_id_type=MESH)
    copies = [pltpu.make_async_copy(source, target, local.at[k]) for k, (source, target) in enumerate(zip((s_all, d_all, c_all), shared[5][:3]))]
    for copy in copies:
        copy.start()
    for copy in copies:
        copy.wait()
    pl.semaphore_wait(barrier, 2)
    unpack_and_encode(cplan, splan, shared, lambda stage: None)


def gather_weights(common_master, split_master, pix, pos, cplan, splan):
    s_own, c_own = align(common_master, split_master, cplan, splan)
    any_spec = pl.BlockSpec(memory_space=pl.ANY)
    vmem = pl.BlockSpec(memory_space=pltpu.VMEM)
    scratch = unpack_scratch(cplan, splan)
    fd = first_dec(splan)
    out_specs = [any_spec] * len(OUT_NAMES) + [vmem] * (3 + NSAVED)
    params = pltpu.CompilerParams(collective_id=0, has_side_effects=True, vmem_limit_bytes=64000 * 1024)
    if cplan.parts == 8 and splan.parts == 8:
        results = pl.pallas_call(
            functools.partial(gather_kernel, cplan, splan),
            out_shape=GATHERED, in_specs=[vmem] * 4, out_specs=out_specs,
            scratch_shapes=scratch + [pltpu.SemaphoreType.DMA((56,)), pltpu.SemaphoreType.DMA((56,)), pltpu.SemaphoreType.DMA((2,))],
            compiler_params=params, name="gather",
        )(s_own, c_own, pix, pos)
    else:
        y = lax.axis_index(TENSOR) // 2
        s_all = lax.all_gather(lax.all_gather(s_own, DP), TENSOR).reshape(2, 2, splan.parts, splan.rows, LANES)
        c_all = jnp.moveaxis(lax.all_gather(lax.all_gather(c_own, DP), TENSOR), 0, 1).reshape(cplan.parts, cplan.rows, LANES)
        s_mine = lax.dynamic_index_in_dim(s_all, y, 0, False)
        d_other = lax.dynamic_index_in_dim(s_all, 1 - y, 0, False)[:, fd:]
        results = pl.pallas_call(
            functools.partial(local_unpack_kernel, cplan, splan),
            out_shape=GATHERED, in_specs=[any_spec] * 3 + [vmem] * 2, out_specs=out_specs,
            scratch_shapes=scratch + [pltpu.SemaphoreType.DMA((3,))], compiler_params=params, name="unpack",
        )(s_mine, d_other, c_all, pix, pos)
    weights = Namespace(**dict(zip(OUT_NAMES, results)))
    small, bias, dbias = results[len(OUT_NAMES) : len(OUT_NAMES) + 3]
    at = 0
    rows = []
    for _, count in SMALLS:
        rows.append(small[at : at + count])
        at += round_up(count, 8)
    a, b, qkv_rows, head_rows = rows
    weights.embedding_bias = a[:6].reshape(1, D)
    weights.enc_norms = a[6:42].reshape(6, D)
    weights.enc_biases = a[42:54].reshape(2, D)
    weights.mask_token = b[:3].reshape(1, DD)
    weights.dec_norms = b[3:21].reshape(6, DD)
    weights.dec_biases = b[21:27].reshape(2, DD)
    weights.dec_qkv_bias = qkv_rows.reshape(2, DD)
    weights.head_bias = head_rows.reshape(1, PATCH)
    weights.enc_qkv_bias = bias[:, :3].reshape(2, 2, 192)
    weights.enc_up_bias = bias[:, 8:14].reshape(1, 1536)
    weights.dec_up_bias = dbias[:, :3].reshape(1, 1536)
    return weights, Namespace(**dict(zip(vars(SAVED), results[len(OUT_NAMES) + 3 :])))


DEC_FIRST = floor16(DEC_ROW)
S_WIDE = round_up(SPLIT_ROWS, TILE)
C_WIDE = round_up(COMMON_ROWS, TILE)
D_WIDE = S_WIDE - DEC_FIRST
SLOTS = 3


def buffer_rows(plan, wide):
    return max(wide, plan.base[-1] + plan.rows)


def narrow(wide, target, count, chunk=128):
    def body(index, _):
        at = pl.ds(pl.multiple_of(index * chunk, TILE), chunk)
        target[at, :] = wide[at, :].astype(BF16)
        return 0

    whole = count // chunk
    lax.fori_loop(0, whole, body, 0)
    if count % chunk:
        target[whole * chunk : count, :] = wide[whole * chunk : count, :].astype(BF16)


def clear(wide, first, last, chunk=64):
    def body(index, _):
        wide[pl.ds(first + index * chunk, chunk), :] = jnp.zeros((chunk, LANES), F32)
        return 0

    whole = (last - first) // chunk
    lax.fori_loop(0, whole, body, 0)
    rest = (last - first) % chunk
    if rest:
        wide[pl.ds(first + whole * chunk, rest), :] = jnp.zeros((rest, LANES), F32)


def matrix_in(wide, start, per_row, stage, rows, width, j0, step=64):
    def body(index, _):
        at = index * step
        for j in range(width // LANES):
            wide[pl.ds(start + j0 + j + at * per_row, step, stride=per_row), :] = stage[
                pl.ds(pl.multiple_of(at, 8), step), j * LANES : (j + 1) * LANES
            ]
        return 0

    lax.fori_loop(0, rows // step, body, 0)


def qkv_in(wide, start, pair_buf, stage):
    step = 32
    lane = lax.broadcasted_iota(jnp.int32, (step, LANES), 1)

    def body(index, _):
        at = start + index * step * 9
        even, odd = [], []
        base = pl.multiple_of(index * 64, 8)
        for j in range(5):
            lanes = slice(j * LANES, (j + 1) * LANES) if j < 4 else slice(512, 640)
            pair_buf[j] = stage[pl.ds(base, 64), lanes]
            even.append(pair_buf[j, pl.ds(0, step, stride=2), :])
            odd.append(pltpu.roll(pair_buf[j, pl.ds(1, step, stride=2), :], 64, 1))
        for j in range(4):
            wide[pl.ds(at + j, step, stride=9), :] = even[j]
        wide[pl.ds(at + 4, step, stride=9), :] = jnp.where(lane < 64, even[4], odd[0])
        for j in range(4):
            wide[pl.ds(at + 5 + j, step, stride=9), :] = jnp.where(lane < 64, odd[j], odd[j + 1])
        return 0

    lax.fori_loop(0, 12, body, 0)


def add_rows(target, parts, count, chunk=None):
    chunk = chunk or max(c for c in (128, 64, 48, 32, 16) if count % c == 0)

    def body(index, _):
        at = index * chunk
        total = None
        for ref, start in parts:
            value = ref[pl.ds(pl.multiple_of(start + at, TILE), chunk), :].astype(F32)
            total = value if total is None else total + value
        target[pl.ds(pl.multiple_of(at, TILE), chunk), :] = total.astype(target.dtype)
        return 0

    lax.fori_loop(0, count // chunk, body, 0)


def unalign(source, target, share, offset):
    down, lanes = offset // LANES, offset % LANES
    step = 64
    lane = lax.broadcasted_iota(jnp.int32, (step, LANES), 1)
    row = lax.broadcasted_iota(jnp.int32, (step, LANES), 0)

    def body(index, total):
        at = index * step
        here = pltpu.roll(source[pl.ds(down + at, step), :], LANES - lanes, 1)
        after = pltpu.roll(source[pl.ds(down + at + 1, step), :], LANES - lanes, 1)
        value = jnp.where(lane < LANES - lanes, here, after)
        value = jnp.where((row + at) * LANES + lane < share, value, 0.0)
        target[pl.ds(pl.multiple_of(at, 8), step), :] = value
        square = (value * value).reshape(step // 8, 8, LANES)
        return total + jnp.sum(square, axis=0)

    return lax.fori_loop(0, target.shape[0] // step, body, jnp.zeros((8, LANES), F32))


def flat_rows(share):
    return round_up(-(-share // LANES), 64)


def grad_jobs(y, grads, small, bias, dbias, wide, pair_buf, gs, gd, gc):
    grad = Namespace(**dict(zip(OUT_NAMES, grads)))
    half = CROW.embedding[1] // 2

    def matrix(source, rows, width, per_row, start, j0=0):
        def place(stage):
            matrix_in(wide, start, per_row, stage, rows, width, j0)

        return (place, source, rows, width)

    def small_rows(source, start):
        def action():
            wide[pl.ds(start, source.shape[0]), :] = source[...]

        return (action,)

    def columns(slot, width):
        return pl.ds(pl.multiple_of(slot * width, LANES), width)

    def rows_of(slot, count):
        return pl.ds(pl.multiple_of(slot * count, 8), count)

    def dec_part(slot, first):
        return [
            matrix(grad.dec_up.at[:, columns(slot, 384)], DD, 384, 3, SROW.dec_up[0] - first),
            small_rows(dbias.at[slot, pl.ds(0, 3)], SROW.dec_up_bias[0] - first),
            matrix(grad.dec_down.at[rows_of(slot, 384)], 384, DD, 3, SROW.dec_down[0] - first),
            (functools.partial(clear, wide, SPLIT_ROWS - first, S_WIDE - first),)]

    def split_jobs(slot):
        return [
            (functools.partial(qkv_in, wide, SROW.enc_qkv[0], pair_buf), grad.enc_qkv.at[:, columns(slot, 640)], D, 640),
            small_rows(bias.at[slot, pl.ds(0, 3)], SROW.enc_qkv_bias[0]),
            matrix(grad.enc_proj.at[rows_of(slot, 192)], 192, D, 6, SROW.enc_proj[0]),
            matrix(grad.enc_up.at[:, columns(slot, 768)], D, 768, 6, SROW.enc_up[0]),
            small_rows(bias.at[slot, pl.ds(8, 6)], SROW.enc_up_bias[0]),
            matrix(grad.enc_down.at[rows_of(slot, 768)], 768, D, 6, SROW.enc_down[0]),
        ] + dec_part(slot, 0) + [(lambda: narrow(wide, gs.at[slot], S_WIDE),)]

    def dec_jobs(slot):
        return [(lambda: clear(wide, 0, DEC_ROW - DEC_FIRST),)] + dec_part(slot + 2, DEC_FIRST) + [(lambda: narrow(wide, gd.at[slot], D_WIDE),)]

    def clear_other():
        def body(index, _):
            wide[pl.ds((1 - y) * half + index * 64, 64), :] = jnp.zeros((64, LANES), F32)
            return 0

        lax.fori_loop(0, half // 64, body, 0)
        clear(wide, COMMON_ROWS, C_WIDE)

    common = [(clear_other,), matrix(grad.embedding, 768, D, 6, y * half)]
    at = 0
    for start, count in SMALLS:
        common.append(small_rows(small.at[pl.ds(at, count)], start))
        at += round_up(count, 8)
    for name in CMATS[1:]:
        rows, total = vars(OUTS)[name]
        for col in range(0, total, 768):
            width = min(768, total - col)
            common.append(matrix(vars(grad)[name].at[:, pl.ds(col, width)], rows, width, total // LANES, vars(CROW)[name][0], col // LANES))
    common.append((lambda: narrow(wide, gc, C_WIDE),))
    return split_jobs, dec_jobs, common


def run_jobs(jobs, stage, stage_sem):
    loads = [job for job in jobs if len(job) > 1]
    copies = [
        pltpu.make_async_copy(job[1], stage.at[n % SLOTS, pl.ds(0, job[2]), pl.ds(0, job[3])], stage_sem.at[n % SLOTS]) for n, job in enumerate(loads)]
    for copy in copies[: SLOTS - 1]:
        copy.start()
    index = 0
    for job in jobs:
        if len(job) == 1:
            job[0]()
            continue
        if index + SLOTS - 1 < len(copies):
            copies[index + SLOTS - 1].start()
        copies[index].wait()
        job[0](stage.at[index % SLOTS])
        index += 1


ZORDER = (0, 3, 1, 2)
SUBS = 4


def reduce_kernel(cplan, splan, *refs):
    nin = len(OUT_NAMES)
    grads, (small, bias, dbias, loss) = refs[:nin], refs[nin : nin + 4]
    g_split, g_common, sums = refs[nin + 4 : nin + 7]
    (wide, pair_buf, stage, gs, gd, gc, ks, xs, zs, kc, yc, xc, zc, kd, yd, cq, fin, finc, part, stage_sem, send, recv) = refs[nin + 7 :]
    me, t = lax.axis_index(DP), lax.axis_index(TENSOR)
    z, x, y, c = me // 2, me % 2, t // 2, t % 2
    rank = me * 4 + t
    srows, quarter = splan.rows, cplan.rows // 4
    sub = srows // SUBS
    updev, downdev = {DP: (z + 1) % 4 * 2 + x, TENSOR: t}, {DP: (z + 3) % 4 * 2 + x, TENSOR: t}
    xdev, ydev, kdev = {DP: z * 2 + (1 - x), TENSOR: t}, {DP: me, TENSOR: (1 - y) * 2 + c}, {DP: me, TENSOR: y * 2 + (1 - c)}
    others = [(rank + k) % 32 for k in range(1, 32)]
    devices = [{DP: other // 4, TENSOR: other % 4} for other in others]
    barrier = pltpu.get_barrier_semaphore()
    for device in devices:
        pl.semaphore_signal(barrier, inc=1, device_id=device, device_id_type=MESH)

    def remote(source, target, slot, device):
        return pltpu.make_async_remote_copy(
            src_ref=source, dst_ref=target, send_sem=send.at[slot], recv_sem=recv.at[slot], device_id=device, device_id_type=MESH)

    def s_at(i):
        return pl.multiple_of(i * splan.share // BLOCK * TILE, TILE)

    def c_at(i, tt):
        return pl.multiple_of(i * cplan.share // BLOCK * TILE + tt * quarter, TILE)

    def piece(q):
        return pl.ds(pl.multiple_of(q * sub, TILE), sub)

    def kd_copy():
        return remote(gd.at[1 - c], kd, 0, kdev)

    def ks_copy(i):
        return remote(gs.at[1 - c, pl.ds(s_at(i), srows)], ks.at[i], 1 + i, kdev)

    def kc_copy(i, yy):
        return remote(gc.at[pl.ds(c_at(i, 2 * yy + 1 - c), quarter)], kc.at[i, yy], 9 + i * 2 + yy, kdev)

    def yd_copy():
        return remote(kd, yd, 25, ydev)

    def yc_copy(i):
        return remote(kc.at[i, 1 - y], yc.at[i], 26 + i, ydev)

    def xs_copy(zz, q):
        return remote(ks.at[zz * 2 + (1 - x), piece(q)], xs.at[zz, piece(q)], 34 + zz * 4 + q, xdev)

    def xc_copy(zz):
        return remote(yc.at[zz * 2 + (1 - x)], xc.at[zz], 50 + zz, xdev)

    def zs_copy(down, zz, q):
        return remote(xs.at[zz, piece(q)], zs.at[down, zz, piece(q)], 54 + down * 16 + zz * 4 + q, downdev if down else updev)

    def zc_copy(down, zz):
        return remote(xc.at[zz], zc.at[down, zz], 86 + down * 4 + zz, downdev if down else updev)

    def along_z(zz, copy_of, add):
        for down in (0, 1):
            passes = z > zz if down else z < zz
            first = z == 3 if down else z == 0

            @pl.when(jnp.logical_and(passes, first))
            def _():
                add(None)

            @pl.when(jnp.logical_and(passes, jnp.logical_not(first)))
            def _(down=down):
                copy_of(down).wait_recv()
                add(down)

            @pl.when(passes)
            def _(down=down):
                copy_of(down).start()

    def across_x(zz):
        i = zz * 2 + (1 - x)
        ks_copy(i).wait_recv()

        def body(q, _):
            add_rows(ks.at[i, piece(q)], [(ks.at[i, piece(q)], 0), (gs.at[c], s_at(i) + q * sub)], sub)
            xs_copy(zz, q).start()
            return 0

        lax.fori_loop(0, SUBS, body, 0)

    def first_sends():
        pl.semaphore_wait(barrier, 31)
        kd_copy().start()

    def core_sends():
        for zz in ZORDER:
            ks_copy(zz * 2 + (1 - x)).start()
        for zz in ZORDER:
            ks_copy(zz * 2 + x).start()

    def dec_across():
        kd_copy().wait_recv()
        add_rows(kd, [(gd.at[c], 0), (kd, 0)], D_WIDE)
        yd_copy().start()

    def common_core_sends():
        for zz in ZORDER:
            for xx in (0, 1):
                for yy in (0, 1):
                    kc_copy(zz * 2 + xx, yy).start()

    split_jobs, dec_jobs, common_jobs = grad_jobs(y, grads, small, bias, dbias, wide, pair_buf, gs, gd, gc)
    run_jobs(
        dec_jobs(1 - c) + [(first_sends,)] + dec_jobs(c) + split_jobs(1 - c) + [(core_sends,), (dec_across,)] + split_jobs(c)
        + [(functools.partial(across_x, ZORDER[0]),)] + common_jobs + [(common_core_sends,)], stage, stage_sem)
    yd_copy().wait_recv()
    dec_rows = gs.at[c, pl.ds(DEC_FIRST, D_WIDE)]
    add_rows(dec_rows, [(dec_rows, 0), (yd, 0)], D_WIDE)
    for zz in ZORDER[1:]:
        across_x(zz)
    for zz in ZORDER:
        for xx in (0, 1):
            i = zz * 2 + xx
            for yy in (0, 1):
                kc_copy(i, yy).wait_recv()
            add_rows(kc.at[i, 1 - y], [(gc, c_at(i, 2 * (1 - y) + c)), (kc.at[i, 1 - y], 0)], quarter)
            yc_copy(i).start()
    for zz in ZORDER:
        i = zz * 2 + (1 - x)
        yc_copy(i).wait_recv()
        add_rows(yc.at[i], [(gc, c_at(i, t)), (kc.at[i, y], 0), (yc.at[i], 0)], quarter)
        xc_copy(zz).start()
        i = zz * 2 + x
        ks_copy(i).wait_recv()

        def body(q, _, zz=zz, i=i):
            xs_copy(zz, q).wait_recv()

            def add(flow):
                parts = [(xs.at[zz, piece(q)], 0), (gs.at[c], s_at(i) + q * sub), (ks.at[i, piece(q)], 0)]
                add_rows(xs.at[zz, piece(q)], parts + ([] if flow is None else [(zs.at[flow, zz, piece(q)], 0)]), sub)

            along_z(zz, lambda down: zs_copy(down, zz, q), add)
            return 0

        lax.fori_loop(0, SUBS, body, 0)
    for zz in ZORDER:
        i = zz * 2 + x
        yc_copy(i).wait_recv()
        xc_copy(zz).wait_recv()

        def add_common(flow, zz=zz, i=i):
            parts = [(xc.at[zz], 0), (gc, c_at(i, t)), (kc.at[i, y], 0), (yc.at[i], 0)]
            add_rows(xc.at[zz], parts + ([] if flow is None else [(zc.at[flow, zz], 0)]), quarter)

        along_z(zz, lambda down, zz=zz: zc_copy(down, zz), add_common)

    def ends(copy_of, action):
        for low, high in ((0, 1), (1, 1), (1, 0)):
            here = jnp.logical_and((z > 0) == bool(low), (z < 3) == bool(high))

            @pl.when(here)
            def _(low=low, high=high):
                flows = [0] * low + [1] * high
                for flow in flows:
                    copy_of(flow)
                action(flows)

    mine = pl.ds(pl.multiple_of(t * quarter, TILE), quarter)
    ends(
        lambda flow: zc_copy(flow, z).wait_recv(),
        lambda flows: add_rows(
            cq.at[mine], [(xc.at[z], 0), (gc, c_at(me, t)), (kc.at[me, y], 0), (yc.at[me], 0)] + [(zc.at[flow, z], 0) for flow in flows], quarter))
    far = pl.ds(pl.multiple_of(((1 - y) * 2 + c) * quarter, TILE), quarter)
    across_t, beside_t, beside_far = remote(cq.at[mine], cq.at[mine], 94, ydev), remote(cq.at[mine], cq.at[mine], 95, kdev), remote(cq.at[far], cq.at[far], 96, kdev)
    across_t.start()
    beside_t.start()

    def wait_split(flow):
        for q in range(SUBS):
            zs_copy(flow, z, q).wait_recv()

    ends(
        wait_split,
        lambda flows: add_rows(fin, [(xs.at[z], 0), (gs.at[c], s_at(me)), (ks.at[me], 0)] + [(zs.at[flow, z], 0) for flow in flows], srows))
    across_t.wait_recv()
    beside_far.start()
    squares = unalign(fin, g_split, splan.share, me * splan.share % BLOCK)
    beside_t.wait_recv()
    beside_far.wait_recv()
    add_rows(finc, [(cq, 0)], cplan.rows)
    squares += unalign(finc, g_common, cplan.share, me * cplan.share % BLOCK) * 0.25
    part[rank, 0:8, :] = squares
    part[rank, 8:16, :] = loss[...]
    shared = [remote(part.at[rank], part.at[rank], 97 + k, device) for k, device in enumerate(devices)]
    for copy in shared:
        copy.start()
    kd_copy().wait_send()
    yd_copy().wait_send()
    for i in range(8):
        ks_copy(i).wait_send()
        yc_copy(i).wait_send()
        for yy in range(2):
            kc_copy(i, yy).wait_send()
    for zz in range(4):
        xc_copy(zz).wait_send()
        for q in range(SUBS):
            xs_copy(zz, q).wait_send()
        for down in (0, 1):
            @pl.when(z > zz if down else z < zz)
            def _(down=down, zz=zz):
                zc_copy(down, zz).wait_send()
                for q in range(SUBS):
                    zs_copy(down, zz, q).wait_send()
    for copy in (across_t, beside_t, beside_far):
        copy.wait_send()
    for copy in shared:
        copy.wait_recv()

    def total(index, value):
        return value + part[index]

    sums[...] = lax.fori_loop(0, 32, total, jnp.zeros((16, LANES), F32))
    for copy in shared:
        copy.wait_send()


def pack_kernel(*refs):
    nin = len(OUT_NAMES)
    grads, (small, bias, dbias) = refs[:nin], refs[nin : nin + 3]
    gs_out, gd_out, gc_out = refs[nin + 3 : nin + 6]
    wide, pair_buf, stage, gs, gd, gc, stage_sem, out_sem = refs[nin + 6 :]
    split_jobs, dec_jobs, common_jobs = grad_jobs(lax.axis_index(TENSOR) // 2, grads, small, bias, dbias, wide, pair_buf, gs, gd, gc)
    run_jobs(dec_jobs(0) + dec_jobs(1) + split_jobs(0) + split_jobs(1) + common_jobs, stage, stage_sem)
    copies = [pltpu.make_async_copy(a, b, out_sem.at[k]) for k, (a, b) in enumerate(((gs, gs_out), (gd, gd_out), (gc, gc_out)))]
    for copy in copies:
        copy.start()
    for copy in copies:
        copy.wait()


def unalign_kernel(share_s, share_c, scalars, s_in, c_in, s_out, c_out, sums):
    sums[...] = unalign(s_in, s_out, share_s, scalars[0]) + unalign(c_in, c_out, share_c, scalars[1]) * 0.25


def reduce_grads(grads, small, bias, dbias, loss, cplan, splan):
    any_spec, vmem = pl.BlockSpec(memory_space=pl.ANY), pl.BlockSpec(memory_space=pltpu.VMEM)
    srows, quarter = splan.rows, cplan.rows // 4
    gs_rows, gc_rows = buffer_rows(splan, S_WIDE), buffer_rows(cplan, C_WIDE)
    flat = (jax.ShapeDtypeStruct((flat_rows(splan.share), LANES), F32), jax.ShapeDtypeStruct((flat_rows(cplan.share), LANES), F32))
    packing = [
        pltpu.VMEM((C_WIDE, LANES), F32), pltpu.VMEM((5, 64, LANES), F32), pltpu.VMEM((SLOTS, 768, 768), F32),
        pltpu.VMEM((2, gs_rows, LANES), BF16), pltpu.VMEM((2, D_WIDE, LANES), BF16), pltpu.VMEM((gc_rows, LANES), BF16)]
    operands = [vars(grads)[name] for name in OUT_NAMES]
    limit = 67_000_000
    if cplan.parts == 8 and splan.parts == 8:
        def rows(*shape, kind=BF16):
            return pltpu.VMEM(shape + (LANES,), kind)

        copies = 128
        return pl.pallas_call(
            functools.partial(reduce_kernel, cplan, splan),
            out_shape=flat + (jax.ShapeDtypeStruct((16, LANES), F32),),
            in_specs=[any_spec] * len(operands) + [vmem] * 4, out_specs=[vmem] * 3,
            scratch_shapes=packing + [
                rows(8, srows), rows(4, srows), rows(2, 4, srows), rows(8, 2, quarter), rows(8, quarter), rows(4, quarter), rows(2, 4, quarter),
                rows(D_WIDE), rows(D_WIDE), rows(cplan.rows),
                rows(srows + 64, kind=F32), rows(cplan.rows + 64, kind=F32), rows(32, 16, kind=F32),
                pltpu.SemaphoreType.DMA((SLOTS,)), pltpu.SemaphoreType.DMA((copies,)), pltpu.SemaphoreType.DMA((copies,))],
            compiler_params=pltpu.CompilerParams(collective_id=1, has_side_effects=True, vmem_limit_bytes=limit),
            name="reduce",
        )(*operands, small, bias, dbias, loss)
    shapes = [jax.ShapeDtypeStruct((2, gs_rows, LANES), BF16), jax.ShapeDtypeStruct((2, D_WIDE, LANES), BF16), jax.ShapeDtypeStruct((gc_rows, LANES), BF16)]
    gs, gd, gc = pl.pallas_call(
        pack_kernel, out_shape=shapes, in_specs=[any_spec] * len(operands) + [vmem] * 3, out_specs=[any_spec] * 3,
        scratch_shapes=packing + [pltpu.SemaphoreType.DMA((SLOTS,)), pltpu.SemaphoreType.DMA((3,))],
        compiler_params=pltpu.CompilerParams(vmem_limit_bytes=limit), name="pack",
    )(*operands, small, bias, dbias)
    me, t = lax.axis_index(DP), lax.axis_index(TENSOR)
    c = t % 2

    def swap(value, bit):
        return lax.ppermute(value, TENSOR, [(i, i ^ bit) for i in range(4)])

    def mine(value):
        keep = lax.dynamic_index_in_dim(value, c, 0, False).astype(F32)
        return keep + swap(lax.dynamic_index_in_dim(value, 1 - c, 0, False), 1).astype(F32)

    far = swap(mine(gd).astype(BF16), 2)
    split_sum = mine(gs).at[DEC_FIRST : DEC_FIRST + D_WIDE].add(far.astype(F32))
    common_sum = lax.psum(gc, TENSOR).astype(F32)

    def scattered(value, plan):
        frames = jnp.stack([value[base : base + plan.rows] for base in plan.base])
        return lax.psum_scatter(frames.astype(BF16), DP, scatter_dimension=0, tiled=True)[0].astype(F32)

    s_frame, c_frame = scattered(split_sum, splan), scattered(common_sum, cplan)
    pad = ((0, 64), (0, 0))
    g_split, g_common, squares = pl.pallas_call(
        functools.partial(unalign_kernel, splan.share, cplan.share), out_shape=flat + (jax.ShapeDtypeStruct((8, LANES), F32),),
        in_specs=[pl.BlockSpec(memory_space=pltpu.SMEM), vmem, vmem], out_specs=[vmem] * 3, name="unalign",
    )(jnp.stack([me * splan.share % BLOCK, me * cplan.share % BLOCK]).astype(jnp.int32), jnp.pad(s_frame, pad), jnp.pad(c_frame, pad))
    return g_split, g_common, lax.psum(jnp.concatenate([squares, loss]), (DP, TENSOR))


OWN = TUBES // 2
KEYS = 392


def head_masks(rows):
    lane = lax.broadcasted_iota(jnp.int32, (rows, LANES), 1)
    return lane < HEAD, lane >= HEAD


def attend_kernel(q_ref, k_ref, v_ref, o_ref, lse_ref, vt_ref, shifted_ref):
    q = q_ref[...]
    vt_ref[...] = v_ref[...].T
    pieces = []
    for head, mask in enumerate(head_masks(OWN)):
        qm = jnp.where(mask, q * SCALE, jnp.zeros_like(q))
        top = None
        for first in range(0, TUBES, KEYS):
            most = jnp.max(nt(k_ref[first : first + KEYS, :], qm), axis=0, keepdims=True)
            top = most if top is None else jnp.maximum(top, most)
        total = None
        qm = jnp.where(mask, q, jnp.zeros_like(q))
        for first in range(0, TUBES, KEYS):
            shifted = jnp.exp(nt(k_ref[first : first + KEYS, :], qm) * SCALE - top)
            part = jnp.sum(shifted, axis=0, keepdims=True)
            total = part if total is None else total + part
            shifted_ref[first : first + KEYS, :] = shifted.astype(BF16)
        pieces.append(nn(vt_ref[head * HEAD : (head + 1) * HEAD, :], shifted_ref[...]) / total)
        lse_ref[0, head : head + 1, :] = top + jnp.log(total)
    o_ref[...] = jnp.concatenate(pieces, axis=0).T


def attend(q, k, v):
    block, whole = pl.BlockSpec((OWN, LANES), lambda h: (0, h)), pl.BlockSpec((TUBES, LANES), lambda h: (0, h))
    return pl.pallas_call(
        attend_kernel, grid=(3,),
        out_shape=(jax.ShapeDtypeStruct((OWN, DD), F32), jax.ShapeDtypeStruct((3, 8, OWN), F32)),
        in_specs=[block, whole, whole], out_specs=[block, pl.BlockSpec((1, 8, OWN), lambda h: (h, 0, 0))],
        scratch_shapes=[pltpu.VMEM((LANES, TUBES), BF16), pltpu.VMEM((TUBES, OWN), BF16)], name="attend",
    )(q, k, v)


def attend_back_kernel(q_ref, k_ref, v_ref, do_ref, o_ref, lse_ref, dq_ref, dk_ref, dv_ref, kt_ref, ds_ref):
    q, do = q_ref[...], do_ref[...]
    kt_ref[...] = k_ref[...].T
    along = (do.astype(F32) * o_ref[...]).T
    pieces = []
    for head, mask in enumerate(head_masks(OWN)):
        qm, dom = jnp.where(mask, q * SCALE, jnp.zeros_like(q)), jnp.where(mask, do, jnp.zeros_like(do))
        delta = jnp.sum(along[head * HEAD : (head + 1) * HEAD], axis=0, keepdims=True)
        lse = lse_ref[0, head : head + 1, :]
        for first in range(0, TUBES, KEYS):
            rows = slice(first, first + KEYS)
            probs = jnp.exp(nt(k_ref[rows, :], qm) - lse)
            dv = nn(probs.astype(BF16), dom)
            ds = (probs * (nt(v_ref[rows, :], dom) - delta)).astype(BF16)
            ds_ref[rows, :] = ds
            dk = nn(ds, qm)
            if head:
                dk_ref[rows, :] += dk
                dv_ref[rows, :] += dv
            else:
                dk_ref[rows, :] = dk
                dv_ref[rows, :] = dv
        pieces.append(nn(kt_ref[head * HEAD : (head + 1) * HEAD, :], ds_ref[...]))
    dq_ref[...] = (jnp.concatenate(pieces, axis=0) * SCALE).T.astype(BF16)


def attend_back(q, k, v, do, o, lse):
    block, whole = pl.BlockSpec((OWN, LANES), lambda h: (0, h)), pl.BlockSpec((TUBES, LANES), lambda h: (0, h))
    return pl.pallas_call(
        attend_back_kernel, grid=(3,),
        out_shape=(jax.ShapeDtypeStruct((OWN, DD), BF16), jax.ShapeDtypeStruct((TUBES, DD), F32), jax.ShapeDtypeStruct((TUBES, DD), F32)),
        in_specs=[block, whole, whole, block, block, pl.BlockSpec((1, 8, OWN), lambda h: (h, 0, 0))], out_specs=[block, whole, whole],
        scratch_shapes=[pltpu.VMEM((LANES, TUBES), BF16), pltpu.VMEM((TUBES, OWN), BF16)], name="attend_back",
    )(q, k, v, do, o, lse)


NORM_EPS = 1e-06
PIXEL_EPS = 1e-06
CLIP_RATIO = 1.5
BETA_FIRST = 0.9
BETA_SECOND = 0.95
LEARN_RATE = 0.05
DECAY_RATE = 0.05
ADAM_EPS = 1e-08


def layer_norm(inputs, gain, shift):
    centered = inputs - jnp.mean(inputs, axis=-1, keepdims=True)
    spread = jnp.mean(centered * centered, axis=-1, keepdims=True)
    return centered * lax.rsqrt(spread + NORM_EPS) * gain + shift


def norm_back(inputs, gain, grad):
    centered = inputs - jnp.mean(inputs, axis=-1, keepdims=True)
    scale = lax.rsqrt(jnp.mean(centered * centered, axis=-1, keepdims=True) + NORM_EPS)
    unit = centered * scale
    inner = grad * gain
    back = scale * (inner - jnp.mean(inner, axis=-1, keepdims=True) - unit * jnp.mean(inner * unit, axis=-1, keepdims=True))
    return back, jnp.sum(grad * unit, axis=0), jnp.sum(grad, axis=0)


def tn(a, b):
    return lax.dot_general(a, b, (((0,), (0,)), ((), ())), preferred_element_type=F32)


def gelu(inputs):
    return jax.nn.gelu(inputs, approximate=False)


def gelu_slope(inputs):
    return 0.5 * (1.0 + lax.erf(inputs * math.sqrt(0.5))) + inputs * jnp.exp(-0.5 * inputs * inputs) * (1.0 / math.sqrt(2.0 * math.pi))


def sine_rows(position, width):
    column = jnp.arange(width)
    exponent = (2 * (column // 2)).astype(F32) / width
    angles = position.astype(F32)[:, None] / jnp.power(10000.0, exponent)[None, :]
    return jnp.where((column % 2 == 0)[None, :], jnp.sin(angles), jnp.cos(angles))


def sine_table(width, step=32):
    column = np.arange(width)
    rate = 10000.0 ** (-(2 * (column // 2)) / width)
    high, low = np.arange(0, TUBES, step)[:, None] * rate, np.arange(step)[:, None] * rate
    even = column % 2 == 0
    a = np.where(even, np.sin(high), np.cos(high)).astype(np.float32)
    b = np.where(even, np.cos(high), -np.sin(high)).astype(np.float32)
    c, s = np.cos(low).astype(np.float32), np.sin(low).astype(np.float32)
    table = a[:, None] * jnp.asarray(c)[None] + b[:, None] * jnp.asarray(s)[None]
    return table.reshape(TUBES, width)


def across(value):
    return lax.ppermute(value, TENSOR, [(i, i ^ 2) for i in range(4)])


def beside(value):
    return lax.ppermute(value, TENSOR, [(i, i ^ 1) for i in range(4)])


def y_total(partial):
    low = partial.astype(BF16)
    return low.astype(F32) + across(low).astype(F32)


def heads_back(parts):
    stacked = jnp.stack([part.reshape(2, 3, VP, HEAD) for part in parts], axis=1)
    return stacked.transpose(3, 0, 1, 2, 4).reshape(VP, 1152)


def seen_inputs(pixels, order):
    c = lax.axis_index(TENSOR) % 2
    seen = jnp.pad(lax.dynamic_index_in_dim(order, c, 0, False)[:VIS], (0, VP - VIS))
    return jnp.take(pixels.reshape(2 * TUBES, PATCH), c * TUBES + seen, axis=0), sine_rows(seen, D)


def step_grads(pixels, order, seen_pixels, w, saved, scale_back):
    t = lax.axis_index(TENSOR)
    y, c = t // 2, t % 2
    first_y = (y == 0).astype(F32)
    seen_y = jnp.pad(lax.dynamic_index_in_dim(order, y, 0, False)[:VIS], (0, VP - VIS), constant_values=-1)
    rows = pixels.reshape(2 * TUBES, PATCH)
    norms = w.enc_norms
    embedded, normed_a, merged, after, normed_m = saved.embedded, saved.normed_a, saved.merged, saved.after, saved.normed_m
    raised, active, encoded, final_low = saved.raised, saved.active, saved.encoded, saved.final_low
    parts = saved.mixed.reshape(2, VP, 3, 3, HEAD)
    q, k, v = [parts[:, :, n].transpose(0, 2, 1, 3).reshape(6, VP, HEAD) for n in range(3)]
    probs = saved.probs
    probs_low = probs.astype(BF16)
    qkv_w = jnp.concatenate([w.enc_qkv[0], w.enc_qkv[1]], axis=1)
    lowered = saved.lowered
    select = seen_y[None, :] == jnp.arange(TUBES, dtype=jnp.int32)[:, None]
    visible = jnp.any(select, axis=1, keepdims=True)
    placed = lax.dot_general(select.astype(F32), lowered, (((1,), (0,)), ((), ())), precision=lax.Precision.HIGHEST, preferred_element_type=F32)
    dec_in = placed + jnp.where(visible, 0.0, w.mask_token) + sine_table(DD)
    start = c * OWN

    def own(value):
        return lax.dynamic_slice_in_dim(value, start, OWN, 0)

    dnorms, dbiases = w.dec_norms, w.dec_biases
    normed_all = layer_norm(dec_in, dnorms[0], dnorms[1]).astype(BF16)
    normed_q = own(normed_all)
    dec_own = own(dec_in)
    query = (nn(normed_q, w.dec_qkv[:, :DD]) + w.dec_qkv_bias[0]).astype(BF16)
    key = nn(normed_all, w.dec_qkv[:, DD : 2 * DD]).astype(BF16)
    value = (nn(normed_all, w.dec_qkv[:, 2 * DD :]) + w.dec_qkv_bias[1]).astype(BF16)
    attended, lse = attend(query, key, value)
    attended_low = attended.astype(BF16)
    mid = dec_own + (nn(attended_low, w.dec_proj) + dbiases[0])
    normed_d = layer_norm(mid, dnorms[2], dnorms[3]).astype(BF16)
    draised = nn(normed_d, w.dec_up) + w.dec_up_bias
    dactive = gelu(draised).astype(BF16)
    decoded = mid + (nn(dactive, w.dec_down) + dbiases[1])
    head_low = layer_norm(decoded, dnorms[4], dnorms[5]).astype(BF16)
    predicted = nn(head_low, w.pixel_head) + w.head_bias
    target = lax.dynamic_slice_in_dim(rows, y * TUBES + start, OWN, 0).astype(F32)
    target = target - jnp.mean(target, axis=-1, keepdims=True)
    target = target * lax.rsqrt(jnp.mean(target * target, axis=-1, keepdims=True) + PIXEL_EPS)
    hidden = 1.0 - own(visible.astype(F32))
    missing = (predicted - target) * hidden
    loss = jnp.sum((missing * missing).reshape(-1, 8, PATCH // LANES, LANES), axis=(0, 2))
    pred_grad = (2.0 * scale_back * missing).astype(BF16)
    grads, small = Namespace(), Namespace()
    grads.pixel_head = tn(head_low, pred_grad)
    small.head_bias = jnp.sum(pred_grad, axis=0, dtype=F32)
    decoded_grad, dg4, dg5 = norm_back(decoded, dnorms[4], nt(pred_grad, w.pixel_head))
    branch = decoded_grad.astype(BF16)
    grads.dec_down = tn(dactive, branch)
    db1 = jnp.sum(branch, axis=0, dtype=F32)
    draised_grad = (nt(branch, w.dec_down) * gelu_slope(draised)).astype(BF16)
    grads.dec_up = tn(normed_d, draised_grad)
    dec_up_bias = jnp.sum(draised_grad, axis=0, dtype=F32)
    back, dg2, dg3 = norm_back(mid, dnorms[2], nt(draised_grad, w.dec_up))
    mid_grad = decoded_grad + back
    branch = mid_grad.astype(BF16)
    grads.dec_proj = tn(attended_low, branch)
    db0 = jnp.sum(branch, axis=0, dtype=F32)
    attended_grad = nt(branch, w.dec_proj).astype(BF16)
    query_grad, key_grad, value_grad = attend_back(query, key, value, attended_grad, attended, lse)

    def shared(total):
        keep = lax.dynamic_slice_in_dim(total, start, OWN, 0)
        give = lax.dynamic_slice_in_dim(total, OWN - start, OWN, 0).astype(BF16)
        return (keep + beside(give).astype(F32)).astype(BF16)

    mixed = jnp.concatenate([query_grad, shared(key_grad), shared(value_grad)], axis=1)
    grads.dec_qkv = tn(normed_q, mixed)
    dqb = jnp.sum(mixed, axis=0, dtype=F32)
    small.dec_qkv_bias = jnp.concatenate([dqb[:DD], dqb[2 * DD :]])
    back, dg0, dg1 = norm_back(dec_own, dnorms[0], nt(mixed, w.dec_qkv))
    in_grad = mid_grad + back
    small.mask_token = jnp.sum(in_grad * hidden, axis=0)
    part = tn(own(select).astype(BF16), in_grad.astype(BF16)).astype(BF16)
    near = lax.ppermute(part, TENSOR, [(1, 0), (2, 3)])
    joined = part + near
    far = lax.ppermute(joined, TENSOR, [(0, 2), (3, 1)])
    lowered_grad = jnp.where(y == c, joined, far)
    grads.to_decoder = tn(final_low, lowered_grad) * first_y
    encoded_grad, eg4, eg5 = norm_back(encoded, norms[4], nt(lowered_grad, w.to_decoder))
    branch = encoded_grad.astype(BF16)
    grads.enc_down = tn(active, branch)
    eb1 = jnp.sum(branch, axis=0, dtype=F32)
    raised_grad = (nt(branch, w.enc_down) * gelu_slope(raised)).astype(BF16)
    grads.enc_up = tn(normed_m, raised_grad)
    enc_up_bias = jnp.sum(raised_grad, axis=0, dtype=F32)
    back, eg2, eg3 = norm_back(after, norms[2], y_total(nt(raised_grad, w.enc_up)))
    after_grad = encoded_grad + back
    branch = after_grad.astype(BF16)
    grads.enc_proj = tn(merged, branch)
    eb0 = jnp.sum(branch, axis=0, dtype=F32)
    merged_grad = nt(branch, w.enc_proj).astype(BF16).reshape(VP, 6, HEAD).transpose(1, 0, 2)
    v_grad = jnp.einsum("hqk,hqe->hke", probs_low, merged_grad, preferred_element_type=F32).astype(BF16)
    probs_grad = jnp.einsum("hqe,hke->hqk", merged_grad, v, preferred_element_type=F32)
    scores_low = (probs * (probs_grad - jnp.sum(probs_grad * probs, axis=-1, keepdims=True))).astype(BF16)
    q_grad = (jnp.einsum("hqk,hke->hqe", scores_low, k, preferred_element_type=F32) * SCALE).astype(BF16)
    k_grad = (jnp.einsum("hqk,hqe->hke", scores_low, q, preferred_element_type=F32) * SCALE).astype(BF16)
    emixed = heads_back([q_grad, k_grad, v_grad])
    wide_mixed = jnp.pad(emixed.reshape(VP, 2, 576), ((0, 0), (0, 0), (0, 64))).reshape(VP, 1280)
    grads.enc_qkv = tn(normed_a, wide_mixed)
    eqb = jnp.sum(emixed, axis=0, dtype=F32).reshape(2, 3, 192)
    back, eg0, eg1 = norm_back(embedded, norms[0], y_total(nt(emixed, qkv_w)))
    embedded_low = (after_grad + back).astype(BF16)
    grads.embedding = tn(lax.dynamic_slice_in_dim(seen_pixels, y * 768, 768, 1), embedded_low)
    embedding_bias = jnp.sum(embedded_low, axis=0, dtype=F32)
    small_a = jnp.concatenate([embedding_bias, eg0, eg1, eg2, eg3, eg4, eg5, eb0, eb1]) * first_y
    small_b = jnp.concatenate([small.mask_token, dg0, dg1, dg2, dg3, dg4, dg5, db0, db1])
    tiles = []
    for piece in (small_a, small_b, small.dec_qkv_bias, small.head_bias):
        count = piece.shape[0] // LANES
        tiles.append(jnp.pad(piece.reshape(count, LANES), ((0, -count % 8), (0, 0))))
    bias = jnp.concatenate(
        [jnp.pad(eqb[:, ::2].reshape(2, 3, LANES), ((0, 0), (0, 5), (0, 0))), jnp.pad(enc_up_bias.reshape(2, 6, LANES), ((0, 0), (0, 2), (0, 0)))], axis=1)
    dbias = jnp.pad(dec_up_bias.reshape(4, 3, LANES), ((0, 0), (0, 5), (0, 0)))
    return loss, grads, jnp.concatenate(tiles), bias, dbias


def adamw(master, first, second, gradient):
    first_new = BETA_FIRST * first + (1.0 - BETA_FIRST) * gradient
    second_new = BETA_SECOND * second + (1.0 - BETA_SECOND) * gradient * gradient
    first_hat = first_new / (1.0 - BETA_FIRST**STEP)
    second_hat = second_new / (1.0 - BETA_SECOND**STEP)
    master_new = master - LEARN_RATE * (first_hat / (jnp.sqrt(second_hat) + ADAM_EPS) + DECAY_RATE * master)
    return (master_new, first_new, second_new, master_new.astype(BF16))


def shards(tubes, tube_order, common_master, common_first, common_second, split_master, split_first, split_second):
    groups = lax.axis_size(DP)
    cplan = Plan(groups, common_master.shape[0], 64)
    splan = Plan(groups, split_master.shape[1], TILE)
    masked_total = tubes.shape[0] * groups * (TUBES - VIS)
    pixel_count = masked_total * PATCH
    seen_pixels, places = seen_inputs(tubes, tube_order)
    w, saved = gather_weights(common_master, split_master, seen_pixels, places, cplan, splan)
    loss, grads, small, bias, dbias = step_grads(tubes, tube_order, seen_pixels, w, saved, 1.0 / pixel_count)
    g_split, g_common, sums = reduce_grads(grads, small, bias, dbias, loss, cplan, splan)
    loss_mean = jnp.sum(sums[8:]) / pixel_count
    grad_norm = jnp.sqrt(jnp.sum(sums[:8]))
    factor = jnp.minimum(1.0, CLIP_RATIO / math.sqrt(masked_total) / (grad_norm + 1e-06))
    common = adamw(common_master, common_first, common_second, g_common.reshape(-1)[: common_master.shape[0]] * factor)
    split = adamw(split_master, split_first, split_second, g_split.reshape(1, -1)[:, : split_master.shape[1]] * factor)
    return (loss_mean.reshape(1), grad_norm.reshape(1)) + common + split


def solution(mesh):
    in_specs = (P(DP, None, None), P(DP, None), P(DP), P(DP), P(DP), P(TENSOR, DP), P(TENSOR, DP), P(TENSOR, DP))
    out_specs = (P(), P()) + (P(DP),) * 4 + (P(TENSOR, DP),) * 4
    return jax.shard_map(shards, mesh=mesh, in_specs=in_specs, out_specs=out_specs, check_vma=False)
```

profile of v0, /device:TPU:0, one launch (start us, length us, event | category | flops | bytes accessed | tf_op | source)
XLA Modules:
  0.0 446.7 jit_solution(10738090440773767480)
XLA Ops:
  0.8 2.6 pad_bitcast_fusion.common_in
  4.2 2.6 pad.48
  6.8 6.4 %gather_fusion = bf16[160,1536]{1,0:T(8,128)(2,1)S(1)} fusion(bf16[3136,1536]{1,0:T(8,128)(2,1)} %bitcast.151, s32[1024]{0:T(1024)S(1)} %pad_clamp_fusion), kind=kCustom, calls=%fused_computation | custom fusion | bytes 983680 | tf_op jit(solution)/shard_map/jit(_take)/gather | solution.py:1299
  13.2 0.9 broadcast_select_fusion.refs_0_
  14.7 3.5 align.1
  18.2 2.6 cosine_select_fusion.refs_1_
  20.8 106.0 %gather.8 = (bf16[1536,768]{1,0:T(8,128)(2,1)}, bf16[768,384]{1,0:T(8,128)(2,1)}, bf16[384,1152]{1,0:T(8,128)(2,1)}, bf16[384,384]{1,0:T(8,128)(2,1)}, bf16[384,...) custom-call(bf16[2048,128]{1,0:T(8,128)(2,1)} %get-tuple-element.44., ...), custom_call_target="tpu_custom_call" | custom-call | tf_op jit(solution)/shard_map/gather/pallas_call | solution.py:610
  126.7 0.9 slice_bitcast_fusion.9
  128.3 1.0 iota_compare_fusion
  129.3 2.1 convert_reduce_fusion
  131.4 2.5 fusion.2
  134.9 2.3 fusion.103
  139.0 1.9 convolution_convert_fusion.k_ref
  140.9 1.4 fusion.31.q_ref
  142.3 1.9 fusion.22.v_ref
  144.3 17.8 %attend.1 = (f32[784,384]{1,0:T(8,128)}, f32[3,8,784]{2,1,0:T(8,128)}) custom-call(bf16[784,384]{1,0:T(8,128)(2,1)} %fusion.31.q_ref, bf16[1568,384]{1,0:T(8,128)(2,1)} %convolution_convert_fusion.k_ref, bf16[1568,384]{1,0:T(8,128)(2,1)} %fusion.22.v_ref), custom_call_target="tpu_custom_call" | custom-call | tf_op jit(solution)/shard_map/attend/pallas_call | solution.py:1178
  162.1 2.1 fusion.104
  164.5 11.4 %fusion.7 = (bf16[784,1536]{1,0:T(8,128)(2,1)S(1)}, f32[784,1536]{1,0:T(8,128)S(1)}) fusion(f32[1536]{0:T(1024)S(1)} %add.393, bf16[384,1536]{1,0:T(8,128)(2,1)S(1)} %copy-done.63, f32[784,384]{1,0:T(8,128)S(1)} %get-tuple-element.156, f32[384]{0:T(512)S(1)} %get-tuple-element.139, f32[384]{0:T(512)S(1)} %get-tuple-element.140, ...), kind=kOutput, calls=%fused_computation.12 | convolution fusion | flops 1005828096 | bytes 9624704 | tf_op jit(solution)/shard_map/dot_general | solution.py:205
  175.9 1.5 fusion.105
  178.1 4.2 convert_reduce_fusion.2
  182.2 2.1 multiply_reduce_fusion.1
  184.4 1.1 convert_reduce_fusion.4
  185.4 3.1 convert_reduce_fusion.1
  188.5 2.2 multiply_reduce_fusion.2
  190.7 1.2 convert_reduce_fusion.5
  191.9 1.0 copy-done.3
  192.9 1.4 convolution_convert_fusion.1.do_ref
  194.3 27.4 %attend_back.1 = (bf16[784,384]{1,0:T(8,128)(2,1)}, f32[1568,384]{1,0:T(8,128)}, f32[1568,384]{1,0:T(8,128)}) custom-call(bf16[784,384]{1,0:T(8,128)(2,1)} %fusion.31.q_ref, bf16[1568,384]{1,0:T(8,128)(2,1)} %convolution_convert_fusion.k_ref, bf16[1568,384]{1,0:T(8,128)(2,1)} %fusion.22.v_ref, bf16[784,384]{1,0:T(8,128)(2,1)} %convolution_convert_fusion.1.do_ref, ...), custom_call_target="tpu_custom_call" | custom-call | tf_op jit(solution)/shard_map/attend_back/pallas_call | solution.py:1214
  221.8 2.3 dynamic-slice_convert_fusion
  224.1 2.3 collective-permute-start.1
  226.4 2.2 dynamic-slice_convert_fusion.1
  228.8 1.4 fusion.56.refs_3_
  230.3 5.5 %fusion.96.refs_4_ = f32[384,1536]{1,0:T(8,128)} fusion(f32[784,384]{1,0:T(8,128)S(1)} %copy-done.8, f32[384]{0:T(512)S(1)} %get-tuple-element.137, f32[384]{0:T(512)S(1)} %get-tuple-element.136, f32[784]{0:T(1024)S(1)} %add_rsqrt_fusion.3, f32[784]{0:T(1024)S(1)} %broadcast_multiply_fusion.10, f32[784,1536]{1,0:T(8,128)} %copy-done), kind=kOutput, calls=%fused_computation.272 | convolution fusion | flops 928757760 | bytes 8389760 | tf_op jit(solution)/shard_map/dot_general | solution.py:1248
  235.8 3.0 fusion.94.refs_9_
  238.8 1.8 bitcast_reduce_fusion.refs_14_
  242.3 1.1 copy.46
  243.3 1.9 fusion.102
  245.3 3.0 slice_bitcast_fusion.1
  249.9 5.4 %fusion.90.refs_10_ = f32[1536,384]{1,0:T(8,128)} fusion(bf16[784,1536]{1,0:T(8,128)(2,1)} %copy-done.66, f32[784,384]{1,0:T(8,128)} %copy-done.14), kind=kOutput, calls=%fused_computation.266 | convolution fusion | flops 925145088 | bytes 5971968 | tf_op jit(solution)/shard_map/dot_general | solution.py:1248
  255.3 1.3 add_convert_fusion.1
  257.2 1.2 add_convert_fusion.2
  258.7 1.9 multiply_reduce_fusion.3
  262.0 1.3 collective-permute-start.2
  263.3 1.9 collective-permute-done.2
  265.4 2.4 collective-permute-start.3
  267.8 2.4 fusion.46.refs_2_
  271.4 0.9 copy-done.62
  272.3 2.4 convert_reduce_fusion.7
  274.7 0.9 convolution_convert_fusion.2
  275.6 1.1 collective-permute-start.4
  276.7 2.9 fusion.107.refs_7_
  279.7 3.0 fusion.85.refs_8_
  282.7 1.4 convolution_multiply_fusion.1.refs_1_
  285.2 1.3 convert_reduce_fusion.9
  289.7 1.0 fusion.32
  290.7 1.0 collective-permute-start.5
  292.1 2.7 fusion.106.refs_5_
  295.4 1.4 fusion.82.refs_6_
  296.8 2.1 collective-permute-done.5
  299.9 1.9 fusion.62.refs_0_
  302.4 125.6 %reduce.2 = (f32[2048,128]{1,0:T(8,128)}, f32[2624,128]{1,0:T(8,128)}, f32[16,128]{1,0:T(8,128)}) custom-call(f32[768,768]{1,0:T(8,128)} %fusion.62.refs_0_, f32[768,384]{1,0:T(8,128)} %convolution_multiply_fusion.1.refs_1_, f32[384,1152]{1,0:T(8,128)} %fusion.46.refs_2_, f32[384,384]{1,0:T(8,128)} %fusion.56.refs_3_, f32[384,1536]{1,0:T(8,128)} %fusion.96.refs_4_, ...), custom_call_target="tpu_custom_call" | custom-call | tf_op jit(solution)/shard_map/reduce/pallas_call | solution.py:1100
  428.0 1.3 slice_reduce_fusion
  430.7 5.5 %fusion.100 = (bf16[333360]{0:T(1024)(128)(2,1)}, f32[333360]{0:T(1024)}, f32[333360]{0:T(1024)}, f32[333360]{0:T(1024)}) fusion(f32[333360]{0:T(1024)} %param.14, f32[]{:T(128)S(6)} %min.3, f32[335872]{0:T(1024)} %bitcast.162, f32[333360]{0:T(1024)} %param.15, f32[333360]{0:T(1024)} %param.16), kind=kLoop, calls=%fused_computation.275 | loop fusion | flops 5667120 | bytes 10000804 | tf_op jit(solution)/shard_map/convert_element_type | solution.py:1429
  436.2 8.0 %fusion.98 = (bf16[1,258240]{1,0:T(2,128)(2,1)}, f32[1,258240]{1,0:T(1,128)}, f32[1,258240]{1,0:T(1,128)}, f32[1,258240]{1,0:T(1,128)}) fusion(f32[1,258240]{1,0:T(1,128)S(1)} %copy-done.18, f32[]{:T(128)S(6)} %min.3, f32[1,262144]{1,0:T(1,128)S(1)} %bitcast.163, f32[1,258240]{1,0:T(1,128)S(1)} %copy-done.28, f32[1,258240]{1,0:T(1,128)S(1)} %copy-done.29), kind=kLoop, calls=%fused_computation.274 | loop fusion | flops 4390080 | bytes 7747204 | tf_op jit(solution)/shard_map/convert_element_type | solution.py:1429
  (226 shorter events, 19.5 us)
Async XLA Ops:
  0.6 3.6 copy-start.17
  131.3 2.6 copy-start.48
  131.4 2.6 copy-start.49
  131.4 2.6 copy-start.50
  131.4 2.6 copy-start.51
  138.4 4.0 copy-start.12
  142.3 1.9 copy-start.56
  144.3 17.8 %copy-start.27 = (bf16[384,384]{1,0:T(8,128)(2,1)S(1)}, bf16[384,384]{1,0:T(8,128)(2,1)}, u32[]{:S(2)}) copy-start(bf16[384,384]{1,0:T(8,128)(2,1)} %get-tuple-element.51) | copy-start | bytes 884740
  162.1 2.4 copy-start.63
  164.2 26.6 %copy-start.1 = (f32[784,384]{1,0:T(8,128)}, f32[784,384]{1,0:T(8,128)S(1)}, u32[]{:S(2)}) copy-start(f32[784,384]{1,0:T(8,128)S(1)} %get-tuple-element.156) | copy-start | bytes 3612676
  164.5 11.4 %copy-start.64 = (bf16[1536,384]{1,0:T(8,128)(2,1)S(1)}, bf16[1536,384]{1,0:T(8,128)(2,1)}, u32[]{:S(2)}) copy-start(bf16[1536,384]{1,0:T(8,128)(2,1)} %get-tuple-element.54) | copy-start | bytes 3538948
  175.9 1.6 copy-start.66
  175.9 2.1 copy-start.26
  177.5 6.9 %copy-start.7 = (f32[784,384]{1,0:T(8,128)}, f32[784,384]{1,0:T(8,128)S(1)}, u32[]{:S(2)}) copy-start(f32[784,384]{1,0:T(8,128)S(1)} %get-tuple-element.160) | copy-start | bytes 3612676
  182.2 2.2 copy-start
  185.4 5.3 %copy-start.14 = (f32[784,384]{1,0:T(8,128)}, f32[784,384]{1,0:T(8,128)S(1)}, u32[]{:S(2)}) copy-start(f32[784,384]{1,0:T(8,128)S(1)} %get-tuple-element.121) | copy-start | bytes 3612676
  188.5 2.2 copy-start.20
  221.8 7.1 %copy-start.4 = (f32[784,384]{1,0:T(8,128)S(1)}, f32[784,384]{1,0:T(8,128)}, u32[]{:S(2)}) copy-start(f32[784,384]{1,0:T(8,128)} %copy-done.3) | copy-start | bytes 3612676
  221.8 7.1 %copy-start.6 = (f32[784,384]{1,0:T(8,128)S(1)}, f32[784,384]{1,0:T(8,128)}, u32[]{:S(2)}) copy-start(f32[784,384]{1,0:T(8,128)} %get-tuple-element.50.o_ref) | copy-start | bytes 3612676
  224.1 31.2 %collective-permute-start.1 = (bf16[784,384]{1,0:T(8,128)(2,1)}, bf16[784,384]{1,0:T(8,128)(2,1)}, u32[]{:S(2)}, u32[]{:S(2)}) collective-permute-start(bf16[784,384]{1,0:T(8,128)(2,1)} %dynamic-slice_convert_fusion), channel_id=1, source_target_pairs={{0,1},{1,0},{2,3},{3,2},{4,5},{5,4},{6,7},{7,6},{8,9},{9,8},{10,11... | collective-permute-start | bytes 1806344 | tf_op jit(solution)/shard_map/ppermute | solution.py:1283
  228.6 1.7 copy-start.8
  228.6 28.1 %collective-permute-start = (bf16[784,384]{1,0:T(8,128)(2,1)}, bf16[784,384]{1,0:T(8,128)(2,1)}, u32[]{:S(2)}, u32[]{:S(2)}) collective-permute-start(bf16[784,384]{1,0:T(8,128)(2,1)} %dynamic-slice_convert_fusion.1), channel_id=1, source_target_pairs={{0,1},{1,0},{2,3},{3,2},{4,5},{5,4},{6,7},{7,6},{8,9},{9,8},{10,11... | collective-permute-start | bytes 1806344 | tf_op jit(solution)/shard_map/ppermute | solution.py:1283
  228.8 10.0 %slice-start = ((s8[4816896]{0:T(1024)(128)(4,1)}), s8[4194304]{0:T(1024)(128)(4,1)S(1)}, s32[]{:S(2)}) async-start(s8[4816896]{0:T(1024)(128)(4,1)} %bitcast.148), calls=%async_computation | async-start | bytes 8388608
  230.3 5.5 %copy-start.2 = (f32[784,384]{1,0:T(8,128)S(1)}, f32[784,384]{1,0:T(8,128)}, u32[]{:S(2)}) copy-start(f32[784,384]{1,0:T(8,128)} %copy-done.1) | copy-start | bytes 3612676
  230.3 5.5 %copy-start.21 = (bf16[784,1536]{1,0:T(8,128)(2,1)S(1)}, bf16[784,1536]{1,0:T(8,128)(2,1)}, u32[]{:S(2)}) copy-start(bf16[784,1536]{1,0:T(8,128)(2,1)} %copy-done.20) | copy-start | bytes 7225348
  230.3 8.5 %slice-start.1 = ((s8[4816896]{0:T(1024)(128)(4,1)}), s8[622592]{0:T(1024)(128)(4,1)S(1)}, s32[]{:S(2)}) async-start(s8[4816896]{0:T(1024)(128)(4,1)} %bitcast.148), calls=%async_computation.1 | async-start | bytes 1245184
  238.8 1.8 copy-start.15
  245.3 3.0 copy-start.10
  249.9 5.4 %copy-start.25 = (f32[1568,384]{1,0:T(8,128)S(1)}, f32[1568,384]{1,0:T(8,128)}, u32[]{:S(2)}) copy-start(f32[1568,384]{1,0:T(8,128)} %get-tuple-element.59) | copy-start | bytes 7225348
  255.3 1.9 copy-start.24
  256.7 1.7 copy-start.39
  256.7 2.0 copy-start.47
  258.7 2.0 copy-start.5
  260.6 7.1 %copy-start.13 = (bf16[1568,384]{1,0:T(8,128)(2,1)S(1)}, bf16[1568,384]{1,0:T(8,128)(2,1)}, u32[]{:S(2)}) copy-start(bf16[1568,384]{1,0:T(8,128)(2,1)} %copy-done.12) | copy-start | bytes 3612676
  262.0 3.2 collective-permute-start.2
  265.2 4.9 %copy-start.52 = (f32[384]{0:T(512)S(1)}, f32[384]{0:T(512)}, u32[]{:S(2)}) copy-start(f32[384]{0:T(512)} %get-tuple-element.87) | copy-start | bytes 4612
  265.3 4.9 %copy-start.53 = (f32[384]{0:T(512)S(1)}, f32[384]{0:T(512)}, u32[]{:S(2)}) copy-start(f32[384]{0:T(512)} %get-tuple-element.120) | copy-start | bytes 4612
  265.3 4.9 %copy-start.54 = (f32[384]{0:T(512)S(1)}, f32[384]{0:T(512)}, u32[]{:S(2)}) copy-start(f32[384]{0:T(512)} %get-tuple-element.122) | copy-start | bytes 4612
  265.3 4.9 %copy-start.58 = (f32[384]{0:T(512)S(1)}, f32[384]{0:T(512)}, u32[]{:S(2)}) copy-start(f32[384]{0:T(512)} %get-tuple-element.82) | copy-start | bytes 4612
  265.3 4.9 %copy-start.59 = (f32[384]{0:T(512)S(1)}, f32[384]{0:T(512)}, u32[]{:S(2)}) copy-start(f32[384]{0:T(512)} %get-tuple-element.88) | copy-start | bytes 4612
  265.3 4.9 %copy-start.60 = (f32[384]{0:T(512)S(1)}, f32[384]{0:T(512)}, u32[]{:S(2)}) copy-start(f32[384]{0:T(512)} %get-tuple-element.78) | copy-start | bytes 4612
  265.3 4.9 %copy-start.61 = (f32[384]{0:T(512)S(1)}, f32[384]{0:T(512)}, u32[]{:S(2)}) copy-start(f32[384]{0:T(512)} %get-tuple-element.89) | copy-start | bytes 4612
  265.3 5.3 %copy-start.16 = (f32[160,768]{1,0:T(8,128)S(1)}, f32[160,768]{1,0:T(8,128)}, u32[]{:S(2)}) copy-start(f32[160,768]{1,0:T(8,128)} %get-tuple-element.46) | copy-start | bytes 1474564
  265.3 5.3 %copy-start.57 = (f32[160]{0:T(256)S(1)}, f32[160]{0:T(256)}, u32[]{:S(2)}) copy-start(f32[160]{0:T(256)} %add_rsqrt_fusion.7) | copy-start | bytes 1924
  265.3 5.3 %copy-start.65 = (bf16[768,384]{1,0:T(8,128)(2,1)S(1)}, bf16[768,384]{1,0:T(8,128)(2,1)}, u32[]{:S(2)}) copy-start(bf16[768,384]{1,0:T(8,128)(2,1)} %get-tuple-element.60) | copy-start | bytes 1769476
  265.4 5.3 %collective-permute-start.3 = (bf16[160,384]{1,0:T(8,128)(2,1)S(1)}, bf16[160,384]{1,0:T(8,128)(2,1)S(1)}, u32[]{:S(2)}, u32[]{:S(2)}) collective-permute-start(bf16[160,384]{1,0:T(8,128)(2,1)S(1)} %add.418), channel_id=1, source_target_pairs={{0,2},{3,1},{4,6},{7,5},{8,10},{11,9},{12,14},{15,13},{16,18},{19,... | collective-permute-start | bytes 368648 | tf_op jit(solution)/shard_map/ppermute | solution.py:1382
  270.6 1.7 copy-start.62
  272.3 2.4 copy-start.22
  274.6 2.1 copy-start.37
  275.6 8.5 %collective-permute-start.4 = (bf16[160,768]{1,0:T(8,128)(2,1)S(1)}, bf16[160,768]{1,0:T(8,128)(2,1)S(1)}, u32[]{:S(2)}, u32[]{:S(2)}) collective-permute-start(bf16[160,768]{1,0:T(8,128)(2,1)S(1)} %convolution_convert_fusion.2), channel_id=1, source_target_pairs={{0,2},{1,3},{2,0},{3,1},{4,6},{5,7},{6,4},{7,5},{8,10},{9,11},{10,... | collective-permute-start | bytes 737288 | tf_op jit(solution)/shard_map/ppermute | solution.py:1279
  276.7 3.0 copy-start.23
  279.7 3.0 copy-start.43
  284.1 2.4 copy-start.40
  285.2 1.8 copy-start.9
  288.2 1.5 copy-start.33
  289.7 2.4 copy-start.42
  290.7 8.1 %collective-permute-start.5 = (bf16[160,768]{1,0:T(8,128)(2,1)S(1)}, bf16[160,768]{1,0:T(8,128)(2,1)S(1)}, u32[]{:S(2)}, u32[]{:S(2)}) collective-permute-start(bf16[160,768]{1,0:T(8,128)(2,1)S(1)} %fusion.32), channel_id=1, source_target_pairs={{0,2},{1,3},{2,0},{3,1},{4,6},{5,7},{6,4},{7,5},{8,10},{9,11},{10,... | collective-permute-start | bytes 737288 | tf_op jit(solution)/shard_map/ppermute | solution.py:1279
  292.1 3.3 copy-start.45
  296.8 3.1 copy-start.19
  299.5 2.3 copy-start.55
  430.7 5.6 %copy-start.18 = (f32[1,258240]{1,0:T(1,128)S(1)}, f32[1,258240]{1,0:T(1,128)}, u32[]{:S(2)}) copy-start(f32[1,258240]{1,0:T(1,128)} %param.17) | copy-start | bytes 3098884
  430.7 5.5 %copy-start.28 = (f32[1,258240]{1,0:T(1,128)S(1)}, f32[1,258240]{1,0:T(1,128)}, u32[]{:S(2)}) copy-start(f32[1,258240]{1,0:T(1,128)} %param.18) | copy-start | bytes 3098884
  430.7 5.5 %copy-start.29 = (f32[1,258240]{1,0:T(1,128)S(1)}, f32[1,258240]{1,0:T(1,128)}, u32[]{:S(2)}) copy-start(f32[1,258240]{1,0:T(1,128)} %param.19) | copy-start | bytes 3098884
  430.7 5.5 %copy-start.30 = (f32[2048,128]{1,0:T(8,128)S(1)}, f32[2048,128]{1,0:T(8,128)}, u32[]{:S(2)}) copy-start(f32[2048,128]{1,0:T(8,128)} %get-tuple-element.77) | copy-start | bytes 3145732
  (11 other events, 11.8 us)
where the time goes:
time: 455 us; the launch traced here: 447 us
  Pallas kernels  280 us (62%)
  matrix products  75.1 us (17%)
  other arithmetic  40.1 us (9%)
  local copies, waits for them, and re-layouts  33.4 us (7%)
  starting transfers between devices  8.19 us (2%)
  between operations  5.76 us (1%)
    pallas_call x1, Pallas kernels, reduce_grads(): pl.pallas_call(functools.partial(reduce_kernel, cplan, splan), out_shape=...  126 us
    pallas_call x1, Pallas kernels, gather_weights(): pl.pallas_call(functools.partial(gather_kernel, cplan, splan), out_shape=...  106 us
    dot_general x12, matrix products, tn(): lax.dot_general(a, b, (((0,), (0,)), ((), ())), preferred_element_type=F32)  31.4 us
    pallas_call x1, Pallas kernels, attend_back(): pl.pallas_call(attend_back_kernel, grid=(3,), out_shape=(jax.ShapeDtypeSt...  27.4 us
    dot_general x7, matrix products, nn(): lax.dot_general(a, b, (((1,), (0,)), ((), ())), preferred_element_type=F32)  24.4 us
    pallas_call x1, Pallas kernels, attend(): pl.pallas_call(attend_kernel, grid=(3,), out_shape=(jax.ShapeDtypeStruct(...  17.8 us
    dot_general x10, matrix products, nt(): lax.dot_general(a, b, (((1,), (1,)), ((), ())), preferred_element_type=F32)  15.9 us
    convert_element_type x2, other arithmetic, adamw(): return (master_new, first_new, second_new, master_new.astype(BF16))  13.5 us
  transfers between devices with their start and end apart: 6, of which 2 were waited for; matrix products, arithmetic and copies ran while one was open for 10% of the time, Pallas kernels for 0%

commit v1 on v0

--- a/solution.py
+++ b/solution.py
@@ -203,6 +203,10 @@
 
 def nn(a, b):
     return lax.dot_general(a, b, (((1,), (0,)), ((), ())), preferred_element_type=F32)
+
+
+def tn(a, b):
+    return lax.dot_general(a, b, (((0,), (0,)), ((), ())), preferred_element_type=F32)
 
 
 VP = 160
@@ -650,23 +654,11 @@
 S_WIDE = round_up(SPLIT_ROWS, TILE)
 C_WIDE = round_up(COMMON_ROWS, TILE)
 D_WIDE = S_WIDE - DEC_FIRST
-SLOTS = 3
+SLOTS = 2
 
 
 def buffer_rows(plan, wide):
     return max(wide, plan.base[-1] + plan.rows)
-
-
-def narrow(wide, target, count, chunk=128):
-    def body(index, _):
-        at = pl.ds(pl.multiple_of(index * chunk, TILE), chunk)
-        target[at, :] = wide[at, :].astype(BF16)
-        return 0
-
-    whole = count // chunk
-    lax.fori_loop(0, whole, body, 0)
-    if count % chunk:
-        target[whole * chunk : count, :] = wide[whole * chunk : count, :].astype(BF16)
 
 
 def clear(wide, first, last, chunk=64):
@@ -754,15 +746,63 @@
     return round_up(-(-share // LANES), 64)
 
 
-def grad_jobs(y, grads, small, bias, dbias, wide, pair_buf, gs, gd, gc):
-    grad = Namespace(**dict(zip(OUT_NAMES, grads)))
-    half = CROW.embedding[1] // 2
+SPLIT_EARLY = round_up(SROW.enc_up[0], TILE)
+SPLIT_LATE = floor16(SROW.enc_up[0])
+COMMON_EARLY = round_up(CROW.to_decoder[0], TILE)
+COMMON_LATE = floor16(CROW.to_decoder[0])
+WIDE_ROWS = max(S_WIDE - SPLIT_LATE, C_WIDE - COMMON_LATE)
+BACK_WEIGHTS = OUT_NAMES[5:9] + OUT_NAMES[1:2]
+LATE_NAMES = OUT_NAMES[2:5] + OUT_NAMES[9:]
+KEPT = tuple(vars(SAVED))[:-1]
+
+
+def norm_rows_back(inputs, gain, grad):
+    centered = inputs - jnp.mean(inputs, axis=-1, keepdims=True)
+    scale = lax.rsqrt(jnp.mean(centered * centered, axis=-1, keepdims=True) + 1e-06)
+    unit = centered * scale
+    inner = grad * gain
+    back = scale * (inner - jnp.mean(inner, axis=-1, keepdims=True) - unit * jnp.mean(inner * unit, axis=-1, keepdims=True))
+    return back, jnp.sum(grad * unit, axis=0, keepdims=True), jnp.sum(grad, axis=0, keepdims=True)
+
+
+def value_in(wide, start, per_row, value, j0=0):
+    rows = value.shape[0]
+    for j in range(value.shape[1] // LANES):
+        wide[pl.ds(start + j0 + j, rows, stride=per_row), :] = value[:, j * LANES : (j + 1) * LANES]
+
+
+def row_in(wide, start, value):
+    for j in range(value.shape[1] // LANES):
+        wide[start + j : start + j + 1, :] = value[:, j * LANES : (j + 1) * LANES]
+
+
+def narrow_part(wide, at, target, row, count, chunk=128):
+    def body(index, _):
+        target[pl.ds(pl.multiple_of(row + index * chunk, TILE), chunk), :] = wide[pl.ds(pl.multiple_of(at + index * chunk, TILE), chunk), :].astype(BF16)
+        return 0
+
+    whole = count // chunk
+    lax.fori_loop(0, whole, body, 0)
+    rest = count % chunk
+    if rest:
+        target[row + whole * chunk : row + count, :] = wide[at + whole * chunk : at + count, :].astype(BF16)
+
+
+def back_and_pack(refs, hooks):
+    (grads, part, seen, norms, small, dbias, weights, saved, wide, pair_buf, stage, stage_sem, gs, gd, gc, held,
+     wq, wp, wu, wd, wt, weight_sem, raised_grad, mixed_grad, deep, swaps, joined, near, send, recv) = refs
+    t = lax.axis_index(TENSOR)
+    me = lax.axis_index(DP)
+    y, c = t // 2, t % 2
+    first_y = jnp.where(y == 0, 1.0, 0.0)
+    ydev, kdev = {DP: me, TENSOR: (1 - y) * 2 + c}, {DP: me, TENSOR: y * 2 + (1 - c)}
+    grad = Namespace(**dict(zip(LATE_NAMES, grads)))
+    loads = [pltpu.make_async_copy(source, target, weight_sem.at[n]) for n, (source, target) in enumerate(zip(weights, (wq, wp, wu, wd, wt)))]
+    for copy in loads:
+        copy.start()
 
     def matrix(source, rows, width, per_row, start, j0=0):
-        def place(stage):
-            matrix_in(wide, start, per_row, stage, rows, width, j0)
-
-        return (place, source, rows, width)
+        return (lambda here: matrix_in(wide, start, per_row, here, rows, width, j0), source, rows, width)
 
     def small_rows(source, start):
         def action():
@@ -783,39 +823,146 @@
             matrix(grad.dec_down.at[rows_of(slot, 384)], 384, DD, 3, SROW.dec_down[0] - first),
             (functools.partial(clear, wide, SPLIT_ROWS - first, S_WIDE - first),)]
 
-    def split_jobs(slot):
-        return [
-            (functools.partial(qkv_in, wide, SROW.enc_qkv[0], pair_buf), grad.enc_qkv.at[:, columns(slot, 640)], D, 640),
-            small_rows(bias.at[slot, pl.ds(0, 3)], SROW.enc_qkv_bias[0]),
-            matrix(grad.enc_proj.at[rows_of(slot, 192)], 192, D, 6, SROW.enc_proj[0]),
-            matrix(grad.enc_up.at[:, columns(slot, 768)], D, 768, 6, SROW.enc_up[0]),
-            small_rows(bias.at[slot, pl.ds(8, 6)], SROW.enc_up_bias[0]),
-            matrix(grad.enc_down.at[rows_of(slot, 768)], 768, D, 6, SROW.enc_down[0]),
-        ] + dec_part(slot, 0) + [(lambda: narrow(wide, gs.at[slot], S_WIDE),)]
-
     def dec_jobs(slot):
-        return [(lambda: clear(wide, 0, DEC_ROW - DEC_FIRST),)] + dec_part(slot + 2, DEC_FIRST) + [(lambda: narrow(wide, gd.at[slot], D_WIDE),)]
-
-    def clear_other():
-        def body(index, _):
-            wide[pl.ds((1 - y) * half + index * 64, 64), :] = jnp.zeros((64, LANES), F32)
-            return 0
-
-        lax.fori_loop(0, half // 64, body, 0)
-        clear(wide, COMMON_ROWS, C_WIDE)
-
-    common = [(clear_other,), matrix(grad.embedding, 768, D, 6, y * half)]
+        return [(lambda: clear(wide, 0, DEC_ROW - DEC_FIRST),)] + dec_part(slot + 2, DEC_FIRST) + [(lambda: narrow_part(wide, 0, gd.at[slot], 0, D_WIDE),)]
+
+    def remote(source, target, slot, device):
+        return pltpu.make_async_remote_copy(
+            src_ref=source, dst_ref=target, send_sem=send.at[slot], recv_sem=recv.at[slot], device_id=device, device_id_type=MESH)
+
+    def norm(k):
+        return jnp.concatenate([norms[6 * k + n : 6 * k + n + 1, :] for n in range(6)], axis=1)
+
+    run_jobs(dec_jobs(1 - c), stage, stage_sem)
+    hooks.first()
+    to_near, to_far = remote(part, near, 0, kdev), remote(joined, joined, 1, ydev)
+
+    @pl.when(y != c)
+    def _():
+        to_near.start()
+
+    run_jobs(dec_jobs(c), stage, stage_sem)
+
+    @pl.when(y == c)
+    def _():
+        to_near.wait_recv()
+        joined[...] = part[...] + near[...]
+        to_far.start()
+
+    for copy in loads:
+        copy.wait()
+
+    @pl.when(y != c)
+    def _():
+        to_far.wait_recv()
+
+    lowered_grad = joined[...]
+    encoded_grad, eg4, eg5 = norm_rows_back(saved.encoded[...], norm(4), nt(lowered_grad, wt[...]))
+    deep[0] = encoded_grad
+    branch = encoded_grad.astype(BF16)
+    eb1 = jnp.sum(branch.astype(F32), axis=0, keepdims=True)
+    for col in range(0, 1536, 384):
+        raised = saved.raised[:, col : col + 384]
+        slope = 0.5 * (1.0 + lax.erf(raised * math.sqrt(0.5))) + raised * jnp.exp(-0.5 * raised * raised) * (1.0 / math.sqrt(2.0 * math.pi))
+        raised_grad[:, col : col + 384] = (nt(branch, wd[col : col + 384, :]) * slope).astype(BF16)
+    swaps[0, 0] = nt(raised_grad[...], wu[...]).astype(BF16)
+    swap = remote(swaps.at[0, 0], swaps.at[0, 1], 2, ydev)
+    swap.start()
+    base = SPLIT_LATE
+    for away in (True, False):
+        slot = 1 - c if away else c
+        cols = columns(slot, 768)
+        value_in(wide, SROW.enc_down[0] - base, 6, tn(saved.active[:, cols], branch))
+        here = raised_grad[:, cols]
+        value_in(wide, SROW.enc_up[0] - base, 6, tn(saved.normed_m[...], here))
+        row_in(wide, SROW.enc_up_bias[0] - base, jnp.sum(here.astype(F32), axis=0, keepdims=True))
+        run_jobs(dec_part(slot, base), stage, stage_sem)
+        held[slot] = wide[0:TILE, :]
+        narrow_part(wide, SPLIT_EARLY - base, gs.at[slot], SPLIT_EARLY, S_WIDE - SPLIT_EARLY)
+        (hooks.early_away if away else hooks.early_own)()
+    swap.wait_recv()
+    back, eg2, eg3 = norm_rows_back(saved.after[...], norm(2), swaps[0, 0].astype(F32) + swaps[0, 1].astype(F32))
+    after_grad = deep[0] + back
+    deep[0] = after_grad
+    branch = after_grad.astype(BF16)
+    eb0 = jnp.sum(branch.astype(F32), axis=0, keepdims=True)
+    merged_grad = nt(branch, wp[...]).astype(BF16)
+    total = None
+    for slot in range(2):
+        pieces = [[], [], []]
+        for head in range(3):
+            q, k, v = [saved.mixed[slot, :, 192 * n + HEAD * head : 192 * n + HEAD * (head + 1)] for n in range(3)]
+            index = slot * 3 + head
+            do = merged_grad[:, index * HEAD : (index + 1) * HEAD]
+            probs = saved.probs[index]
+            pieces[2].append(tn(probs.astype(BF16), do).astype(BF16))
+            dp = nt(do, v)
+            ds = (probs * (dp - jnp.sum(dp * probs, axis=1, keepdims=True))).astype(BF16)
+            pieces[0].append((nn(ds, k) * SCALE).astype(BF16))
+            pieces[1].append((tn(ds, q) * SCALE).astype(BF16))
+        mixed = jnp.concatenate([piece for group in pieces for piece in group] + [jnp.zeros((VP, 64), BF16)], axis=1)
+        mixed_grad[slot] = mixed
+        value = nt(mixed[:, :576], wq[slot])
+        total = value if total is None else total + value
+    swaps[1, 0] = total.astype(BF16)
+    second = remote(swaps.at[1, 0], swaps.at[1, 1], 3, ydev)
+    second.start()
+    for away in (True, False):
+        slot = 1 - c if away else c
+        here = mixed_grad[slot]
+        stage[0, :, 0:640] = tn(saved.normed_a[...], here)
+        qkv_in(wide, SROW.enc_qkv[0], pair_buf, stage.at[0])
+        sums = jnp.sum(here.astype(F32), axis=0, keepdims=True)
+        row_in(wide, SROW.enc_qkv_bias[0], jnp.concatenate([sums[:, :192], sums[:, 384:576]], axis=1))
+        wide[SPLIT_LATE:SPLIT_EARLY, :] = held[slot]
+        mine = jnp.where(slot == 0, saved.merged[:, :192], saved.merged[:, 192:])
+        value_in(wide, SROW.enc_proj[0], 6, tn(mine, branch))
+        narrow_part(wide, 0, gs.at[slot], 0, SPLIT_EARLY)
+        (hooks.late_away if away else hooks.late_own)()
+    base = COMMON_LATE
+    jobs = []
     at = 0
-    for start, count in SMALLS:
-        common.append(small_rows(small.at[pl.ds(at, count)], start))
+    for start, count in SMALLS[1:]:
+        jobs.append(small_rows(small.at[pl.ds(at, count)], start - base))
         at += round_up(count, 8)
-    for name in CMATS[1:]:
-        rows, total = vars(OUTS)[name]
-        for col in range(0, total, 768):
-            width = min(768, total - col)
-            common.append(matrix(vars(grad)[name].at[:, pl.ds(col, width)], rows, width, total // LANES, vars(CROW)[name][0], col // LANES))
-    common.append((lambda: narrow(wide, gc, C_WIDE),))
-    return split_jobs, dec_jobs, common
+    for name in CMATS[2:]:
+        rows, width_all = vars(OUTS)[name]
+        for col in range(0, width_all, 768):
+            width = min(768, width_all - col)
+            jobs.append(matrix(vars(grad)[name].at[:, pl.ds(col, width)], rows, width, width_all // LANES, vars(CROW)[name][0] - base, col // LANES))
+    value_in(wide, CROW.to_decoder[0] - base, 3, tn(saved.final_low[...], lowered_grad) * first_y)
+    clear(wide, COMMON_ROWS - base, C_WIDE - base)
+    run_jobs(jobs, stage, stage_sem)
+    held[0] = wide[0:TILE, :]
+    narrow_part(wide, COMMON_EARLY - base, gc, COMMON_EARLY, C_WIDE - COMMON_EARLY)
+    hooks.common_early()
+    second.wait_recv()
+    back, eg0, eg1 = norm_rows_back(saved.embedded[...], norm(0), swaps[1, 0].astype(F32) + swaps[1, 1].astype(F32))
+    low = (deep[0] + back).astype(BF16)
+    half = CROW.embedding[1] // 2
+
+    def zero(index, _):
+        wide[pl.ds((1 - y) * half + index * 64, 64), :] = jnp.zeros((64, LANES), F32)
+        return 0
+
+    lax.fori_loop(0, half // 64, zero, 0)
+    value_in(wide, y * half, 6, tn(seen[...], low))
+    wide[COMMON_LATE:COMMON_EARLY, :] = held[0]
+    for n, vector in enumerate((jnp.sum(low.astype(F32), axis=0, keepdims=True), eg0, eg1, eg2, eg3, eg4, eg5, eb0, eb1)):
+        row_in(wide, CROW.embedding_bias[0] + 6 * n, vector * first_y)
+    narrow_part(wide, 0, gc, 0, COMMON_EARLY)
+    hooks.common_late()
+
+    @pl.when(y != c)
+    def _():
+        to_near.wait_send()
+
+    @pl.when(y == c)
+    def _():
+        to_far.wait_send()
+
+    swap.wait_send()
+    second.wait_send()
 
 
 def run_jobs(jobs, stage, stage_sem):
@@ -836,15 +983,33 @@
         index += 1
 
 
-ZORDER = (0, 3, 1, 2)
+def back_refs(refs):
+    grads, (part, seen, norms, small, dbias, loss) = refs[: len(LATE_NAMES)], refs[len(LATE_NAMES) : len(LATE_NAMES) + 6]
+    refs = refs[len(LATE_NAMES) + 6 :]
+    weights, kept, outs = refs[:5], refs[5 : 5 + len(KEPT)], refs[5 + len(KEPT) : 8 + len(KEPT)]
+    refs = refs[8 + len(KEPT) :]
+    saved = Namespace(**dict(zip(KEPT, kept)))
+    return (grads, part, seen, norms, small, dbias, weights, saved) + tuple(refs[:22]), loss, outs, refs[22:]
+
+
+def back_scratch(gs_rows, gc_rows):
+    return [
+        pltpu.VMEM((WIDE_ROWS, LANES), F32), pltpu.VMEM((5, 64, LANES), F32), pltpu.VMEM((SLOTS, 768, 768), F32), pltpu.SemaphoreType.DMA((SLOTS,)),
+        pltpu.VMEM((2, gs_rows, LANES), BF16), pltpu.VMEM((2, D_WIDE, LANES), BF16), pltpu.VMEM((gc_rows, LANES), BF16),
+        pltpu.VMEM((2, TILE, LANES), F32),
+    ] + [pltpu.VMEM(vars(OUTS)[name], BF16) for name in BACK_WEIGHTS] + [
+        pltpu.SemaphoreType.DMA((5,)), pltpu.VMEM((VP, 1536), BF16), pltpu.VMEM((2, VP, 640), BF16), pltpu.VMEM((1, VP, D), F32),
+        pltpu.VMEM((2, 2, VP, D), BF16), pltpu.VMEM((VP, DD), BF16), pltpu.VMEM((VP, DD), BF16), pltpu.SemaphoreType.DMA((4,)), pltpu.SemaphoreType.DMA((4,))]
+
+
+ZORDER = (2, 3, 0, 1)
 SUBS = 4
 
 
 def reduce_kernel(cplan, splan, *refs):
-    nin = len(OUT_NAMES)
-    grads, (small, bias, dbias, loss) = refs[:nin], refs[nin : nin + 4]
-    g_split, g_common, sums = refs[nin + 4 : nin + 7]
-    (wide, pair_buf, stage, gs, gd, gc, ks, xs, zs, kc, yc, xc, zc, kd, yd, cq, fin, finc, part, stage_sem, send, recv) = refs[nin + 7 :]
+    back, loss, (g_split, g_common, sums), refs = back_refs(refs)
+    wide, gs, gd, gc = back[8], back[12], back[13], back[14]
+    (ks, xs, zs, kc, yc, xc, zc, kd, yd, cq, part, send, recv) = refs
     me, t = lax.axis_index(DP), lax.axis_index(TENSOR)
     z, x, y, c = me // 2, me % 2, t // 2, t % 2
     rank = me * 4 + t
@@ -927,36 +1092,46 @@
 
         lax.fori_loop(0, SUBS, body, 0)
 
-    def first_sends():
+    def first():
         pl.semaphore_wait(barrier, 31)
         kd_copy().start()
 
-    def core_sends():
-        for zz in ZORDER:
+    def early_away():
+        for zz in ZORDER[:2]:
             ks_copy(zz * 2 + (1 - x)).start()
-        for zz in ZORDER:
+        for zz in ZORDER[:2]:
             ks_copy(zz * 2 + x).start()
-
-    def dec_across():
         kd_copy().wait_recv()
         add_rows(kd, [(gd.at[c], 0), (kd, 0)], D_WIDE)
         yd_copy().start()
 
-    def common_core_sends():
-        for zz in ZORDER:
+    def early_own():
+        across_x(ZORDER[0])
+        yd_copy().wait_recv()
+        dec_rows = gs.at[c, pl.ds(DEC_FIRST, D_WIDE)]
+        add_rows(dec_rows, [(dec_rows, 0), (yd, 0)], D_WIDE)
+        across_x(ZORDER[1])
+
+    def late_away():
+        for zz in ZORDER[2:]:
+            ks_copy(zz * 2 + (1 - x)).start()
+        for zz in ZORDER[2:]:
+            ks_copy(zz * 2 + x).start()
+
+    def late_own():
+        for zz in ZORDER[2:]:
+            across_x(zz)
+
+    def common_core_sends(zzs):
+        for zz in zzs:
             for xx in (0, 1):
                 for yy in (0, 1):
                     kc_copy(zz * 2 + xx, yy).start()
 
-    split_jobs, dec_jobs, common_jobs = grad_jobs(y, grads, small, bias, dbias, wide, pair_buf, gs, gd, gc)
-    run_jobs(
-        dec_jobs(1 - c) + [(first_sends,)] + dec_jobs(c) + split_jobs(1 - c) + [(core_sends,), (dec_across,)] + split_jobs(c)
-        + [(functools.partial(across_x, ZORDER[0]),)] + common_jobs + [(common_core_sends,)], stage, stage_sem)
-    yd_copy().wait_recv()
-    dec_rows = gs.at[c, pl.ds(DEC_FIRST, D_WIDE)]
-    add_rows(dec_rows, [(dec_rows, 0), (yd, 0)], D_WIDE)
-    for zz in ZORDER[1:]:
-        across_x(zz)
+    back_and_pack(back, Namespace(
+        first=first, early_away=early_away, early_own=early_own, late_away=late_away, late_own=late_own,
+        common_early=lambda: common_core_sends(ZORDER[:2]), common_late=lambda: common_core_sends(ZORDER[2:])))
+    fin, finc = wide.at[pl.ds(0, srows + 64)], wide.at[pl.ds(srows + 64, cplan.rows + 64)]
     for zz in ZORDER:
         for xx in (0, 1):
             i = zz * 2 + xx
@@ -1065,13 +1240,19 @@
 
 
 def pack_kernel(*refs):
-    nin = len(OUT_NAMES)
-    grads, (small, bias, dbias) = refs[:nin], refs[nin : nin + 3]
-    gs_out, gd_out, gc_out = refs[nin + 3 : nin + 6]
-    wide, pair_buf, stage, gs, gd, gc, stage_sem, out_sem = refs[nin + 6 :]
-    split_jobs, dec_jobs, common_jobs = grad_jobs(lax.axis_index(TENSOR) // 2, grads, small, bias, dbias, wide, pair_buf, gs, gd, gc)
-    run_jobs(dec_jobs(0) + dec_jobs(1) + split_jobs(0) + split_jobs(1) + common_jobs, stage, stage_sem)
-    copies = [pltpu.make_async_copy(a, b, out_sem.at[k]) for k, (a, b) in enumerate(((gs, gs_out), (gd, gd_out), (gc, gc_out)))]
+    back, _, outs, (out_sem,) = back_refs(refs)
+    t = lax.axis_index(TENSOR)
+    barrier = pltpu.get_barrier_semaphore()
+    for other in (t // 2 * 2 + 1 - t % 2, (1 - t // 2) * 2 + t % 2):
+        pl.semaphore_signal(barrier, inc=1, device_id={DP: lax.axis_index(DP), TENSOR: other}, device_id_type=MESH)
+
+    def nothing():
+        pass
+
+    back_and_pack(back, Namespace(
+        first=lambda: pl.semaphore_wait(barrier, 2), early_away=nothing, early_own=nothing, late_away=nothing, late_own=nothing,
+        common_early=nothing, common_late=nothing))
+    copies = [pltpu.make_async_copy(a, b, out_sem.at[k]) for k, (a, b) in enumerate(zip(back[12:15], outs))]
     for copy in copies:
         copy.start()
     for copy in copies:
@@ -1082,39 +1263,33 @@
     sums[...] = unalign(s_in, s_out, share_s, scalars[0]) + unalign(c_in, c_out, share_c, scalars[1]) * 0.25
 
 
-def reduce_grads(grads, small, bias, dbias, loss, cplan, splan):
+def reduce_grads(grads, part, seen, norms, small, dbias, loss, w, saved, cplan, splan):
     any_spec, vmem = pl.BlockSpec(memory_space=pl.ANY), pl.BlockSpec(memory_space=pltpu.VMEM)
     srows, quarter = splan.rows, cplan.rows // 4
     gs_rows, gc_rows = buffer_rows(splan, S_WIDE), buffer_rows(cplan, C_WIDE)
     flat = (jax.ShapeDtypeStruct((flat_rows(splan.share), LANES), F32), jax.ShapeDtypeStruct((flat_rows(cplan.share), LANES), F32))
-    packing = [
-        pltpu.VMEM((C_WIDE, LANES), F32), pltpu.VMEM((5, 64, LANES), F32), pltpu.VMEM((SLOTS, 768, 768), F32),
-        pltpu.VMEM((2, gs_rows, LANES), BF16), pltpu.VMEM((2, D_WIDE, LANES), BF16), pltpu.VMEM((gc_rows, LANES), BF16)]
-    operands = [vars(grads)[name] for name in OUT_NAMES]
-    limit = 67_000_000
+    operands = [vars(grads)[name] for name in LATE_NAMES] + [part, seen, norms, small, dbias, loss]
+    operands += [vars(w)[name] for name in BACK_WEIGHTS] + [vars(saved)[name] for name in KEPT]
+    in_specs = [any_spec] * len(LATE_NAMES) + [vmem] * 6 + [any_spec] * 5 + [vmem] * len(KEPT)
+    scratch = back_scratch(gs_rows, gc_rows)
+    params = pltpu.CompilerParams(collective_id=1, has_side_effects=True, vmem_limit_bytes=67_000_000)
     if cplan.parts == 8 and splan.parts == 8:
         def rows(*shape, kind=BF16):
             return pltpu.VMEM(shape + (LANES,), kind)
 
-        copies = 128
         return pl.pallas_call(
             functools.partial(reduce_kernel, cplan, splan),
-            out_shape=flat + (jax.ShapeDtypeStruct((16, LANES), F32),),
-            in_specs=[any_spec] * len(operands) + [vmem] * 4, out_specs=[vmem] * 3,
-            scratch_shapes=packing + [
+            out_shape=flat + (jax.ShapeDtypeStruct((16, LANES), F32),), in_specs=in_specs, out_specs=[vmem] * 3,
+            scratch_shapes=scratch + [
                 rows(8, srows), rows(4, srows), rows(2, 4, srows), rows(8, 2, quarter), rows(8, quarter), rows(4, quarter), rows(2, 4, quarter),
-                rows(D_WIDE), rows(D_WIDE), rows(cplan.rows),
-                rows(srows + 64, kind=F32), rows(cplan.rows + 64, kind=F32), rows(32, 16, kind=F32),
-                pltpu.SemaphoreType.DMA((SLOTS,)), pltpu.SemaphoreType.DMA((copies,)), pltpu.SemaphoreType.DMA((copies,))],
-            compiler_params=pltpu.CompilerParams(collective_id=1, has_side_effects=True, vmem_limit_bytes=limit),
-            name="reduce",
-        )(*operands, small, bias, dbias, loss)
+                rows(D_WIDE), rows(D_WIDE), rows(cplan.rows), rows(32, 16, kind=F32), pltpu.SemaphoreType.DMA((128,)), pltpu.SemaphoreType.DMA((128,))],
+            compiler_params=params, name="reduce",
+        )(*operands)
     shapes = [jax.ShapeDtypeStruct((2, gs_rows, LANES), BF16), jax.ShapeDtypeStruct((2, D_WIDE, LANES), BF16), jax.ShapeDtypeStruct((gc_rows, LANES), BF16)]
     gs, gd, gc = pl.pallas_call(
-        pack_kernel, out_shape=shapes, in_specs=[any_spec] * len(operands) + [vmem] * 3, out_specs=[any_spec] * 3,
-        scratch_shapes=packing + [pltpu.SemaphoreType.DMA((SLOTS,)), pltpu.SemaphoreType.DMA((3,))],
-        compiler_params=pltpu.CompilerParams(vmem_limit_bytes=limit), name="pack",
-    )(*operands, small, bias, dbias)
+        pack_kernel, out_shape=shapes, in_specs=in_specs, out_specs=[any_spec] * 3,
+        scratch_shapes=scratch + [pltpu.SemaphoreType.DMA((3,))], compiler_params=params, name="pack",
+    )(*operands)
     me, t = lax.axis_index(DP), lax.axis_index(TENSOR)
     c = t % 2
 
@@ -1244,10 +1419,6 @@
     return back, jnp.sum(grad * unit, axis=0), jnp.sum(grad, axis=0)
 
 
-def tn(a, b):
-    return lax.dot_general(a, b, (((0,), (0,)), ((), ())), preferred_element_type=F32)
-
-
 def gelu(inputs):
     return jax.nn.gelu(inputs, approximate=False)
 
@@ -1275,22 +1446,8 @@
     return table.reshape(TUBES, width)
 
 
-def across(value):
-    return lax.ppermute(value, TENSOR, [(i, i ^ 2) for i in range(4)])
-
-
 def beside(value):
     return lax.ppermute(value, TENSOR, [(i, i ^ 1) for i in range(4)])
-
-
-def y_total(partial):
-    low = partial.astype(BF16)
-    return low.astype(F32) + across(low).astype(F32)
-
-
-def heads_back(parts):
-    stacked = jnp.stack([part.reshape(2, 3, VP, HEAD) for part in parts], axis=1)
-    return stacked.transpose(3, 0, 1, 2, 4).reshape(VP, 1152)
 
 
 def seen_inputs(pixels, order):
@@ -1299,20 +1456,11 @@
     return jnp.take(pixels.reshape(2 * TUBES, PATCH), c * TUBES + seen, axis=0), sine_rows(seen, D)
 
 
-def step_grads(pixels, order, seen_pixels, w, saved, scale_back):
+def step_grads(pixels, order, w, saved, scale_back):
     t = lax.axis_index(TENSOR)
     y, c = t // 2, t % 2
-    first_y = (y == 0).astype(F32)
     seen_y = jnp.pad(lax.dynamic_index_in_dim(order, y, 0, False)[:VIS], (0, VP - VIS), constant_values=-1)
     rows = pixels.reshape(2 * TUBES, PATCH)
-    norms = w.enc_norms
-    embedded, normed_a, merged, after, normed_m = saved.embedded, saved.normed_a, saved.merged, saved.after, saved.normed_m
-    raised, active, encoded, final_low = saved.raised, saved.active, saved.encoded, saved.final_low
-    parts = saved.mixed.reshape(2, VP, 3, 3, HEAD)
-    q, k, v = [parts[:, :, n].transpose(0, 2, 1, 3).reshape(6, VP, HEAD) for n in range(3)]
-    probs = saved.probs
-    probs_low = probs.astype(BF16)
-    qkv_w = jnp.concatenate([w.enc_qkv[0], w.enc_qkv[1]], axis=1)
     lowered = saved.lowered
     select = seen_y[None, :] == jnp.arange(TUBES, dtype=jnp.int32)[:, None]
     visible = jnp.any(select, axis=1, keepdims=True)
@@ -1377,47 +1525,13 @@
     in_grad = mid_grad + back
     small.mask_token = jnp.sum(in_grad * hidden, axis=0)
     part = tn(own(select).astype(BF16), in_grad.astype(BF16)).astype(BF16)
-    near = lax.ppermute(part, TENSOR, [(1, 0), (2, 3)])
-    joined = part + near
-    far = lax.ppermute(joined, TENSOR, [(0, 2), (3, 1)])
-    lowered_grad = jnp.where(y == c, joined, far)
-    grads.to_decoder = tn(final_low, lowered_grad) * first_y
-    encoded_grad, eg4, eg5 = norm_back(encoded, norms[4], nt(lowered_grad, w.to_decoder))
-    branch = encoded_grad.astype(BF16)
-    grads.enc_down = tn(active, branch)
-    eb1 = jnp.sum(branch, axis=0, dtype=F32)
-    raised_grad = (nt(branch, w.enc_down) * gelu_slope(raised)).astype(BF16)
-    grads.enc_up = tn(normed_m, raised_grad)
-    enc_up_bias = jnp.sum(raised_grad, axis=0, dtype=F32)
-    back, eg2, eg3 = norm_back(after, norms[2], y_total(nt(raised_grad, w.enc_up)))
-    after_grad = encoded_grad + back
-    branch = after_grad.astype(BF16)
-    grads.enc_proj = tn(merged, branch)
-    eb0 = jnp.sum(branch, axis=0, dtype=F32)
-    merged_grad = nt(branch, w.enc_proj).astype(BF16).reshape(VP, 6, HEAD).transpose(1, 0, 2)
-    v_grad = jnp.einsum("hqk,hqe->hke", probs_low, merged_grad, preferred_element_type=F32).astype(BF16)
-    probs_grad = jnp.einsum("hqe,hke->hqk", merged_grad, v, preferred_element_type=F32)
-    scores_low = (probs * (probs_grad - jnp.sum(probs_grad * probs, axis=-1, keepdims=True))).astype(BF16)
-    q_grad = (jnp.einsum("hqk,hke->hqe", scores_low, k, preferred_element_type=F32) * SCALE).astype(BF16)
-    k_grad = (jnp.einsum("hqk,hqe->hke", scores_low, q, preferred_element_type=F32) * SCALE).astype(BF16)
-    emixed = heads_back([q_grad, k_grad, v_grad])
-    wide_mixed = jnp.pad(emixed.reshape(VP, 2, 576), ((0, 0), (0, 0), (0, 64))).reshape(VP, 1280)
-    grads.enc_qkv = tn(normed_a, wide_mixed)
-    eqb = jnp.sum(emixed, axis=0, dtype=F32).reshape(2, 3, 192)
-    back, eg0, eg1 = norm_back(embedded, norms[0], y_total(nt(emixed, qkv_w)))
-    embedded_low = (after_grad + back).astype(BF16)
-    grads.embedding = tn(lax.dynamic_slice_in_dim(seen_pixels, y * 768, 768, 1), embedded_low)
-    embedding_bias = jnp.sum(embedded_low, axis=0, dtype=F32)
-    small_a = jnp.concatenate([embedding_bias, eg0, eg1, eg2, eg3, eg4, eg5, eb0, eb1]) * first_y
     small_b = jnp.concatenate([small.mask_token, dg0, dg1, dg2, dg3, dg4, dg5, db0, db1])
     tiles = []
-    for piece in (small_a, small_b, small.dec_qkv_bias, small.head_bias):
+    for piece in (small_b, small.dec_qkv_bias, small.head_bias):
         count = piece.shape[0] // LANES
         tiles.append(jnp.pad(piece.reshape(count, LANES), ((0, -count % 8), (0, 0))))
-    bias = jnp.concatenate(
-        [jnp.pad(eqb[:, ::2].reshape(2, 3, LANES), ((0, 0), (0, 5), (0, 0))), jnp.pad(enc_up_bias.reshape(2, 6, LANES), ((0, 0), (0, 2), (0, 0)))], axis=1)
     dbias = jnp.pad(dec_up_bias.reshape(4, 3, LANES), ((0, 0), (0, 5), (0, 0)))
-    return loss, grads, jnp.concatenate(tiles), bias, dbias
+    return loss, grads, part, jnp.concatenate(tiles), dbias
 
 
 def adamw(master, first, second, gradient):
@@ -1437,8 +1551,9 @@
     pixel_count = masked_total * PATCH
     seen_pixels, places = seen_inputs(tubes, tube_order)
     w, saved = gather_weights(common_master, split_master, seen_pixels, places, cplan, splan)
-    loss, grads, small, bias, dbias = step_grads(tubes, tube_order, seen_pixels, w, saved, 1.0 / pixel_count)
-    g_split, g_common, sums = reduce_grads(grads, small, bias, dbias, loss, cplan, splan)
+    loss, grads, part, small, dbias = step_grads(tubes, tube_order, w, saved, 1.0 / pixel_count)
+    half = lax.dynamic_slice_in_dim(seen_pixels, lax.axis_index(TENSOR) // 2 * 768, 768, 1)
+    g_split, g_common, sums = reduce_grads(grads, part, half, w.enc_norms.reshape(36, LANES), small, dbias, loss, w, saved, cplan, splan)
     loss_mean = jnp.sum(sums[8:]) / pixel_count
     grad_norm = jnp.sqrt(jnp.sum(sums[:8]))
     factor = jnp.minimum(1.0, CLIP_RATIO / math.sqrt(masked_total) / (grad_norm + 1e-06))

time: 455 us -> 432 us (0.949)
  Pallas kernels: 280 us -> 302 us
  matrix products: 75.1 us -> 54.4 us
  local copies, waits for them, and re-layouts: 33.4 us -> 25.1 us
  starting transfers between devices: 8.19 us -> 2.35 us
  other arithmetic: 40.1 us -> 34.5 us
    pallas_call x1, Pallas kernels: 126 us -> 148 us  [reduce_grads(): pl.pallas_call(functools.partial(reduce_kernel, cplan, splan), out_shape=...]
    dot_general x12 -> x6, matrix products: 31.4 us -> 18.7 us  [tn(): lax.dot_general(a, b, (((0,), (0,)), ((), ())), preferred_element_type=F32)]
    dot_general x10 -> x5, matrix products: 15.9 us -> 9.43 us  [nt(): lax.dot_general(a, b, (((1,), (1,)), ((), ())), preferred_element_type=F32)]
    ppermute x4 -> x0, starting transfers between devices: 5.85 us -> none  [the longest x1 2.39 us: step_grads(): far = lax.ppermute(joined, TENSOR, [(0, 2), (3, 1)])]
  transfers between devices with their start and end apart: 6 -> 2, of which waited for: 2 -> 0; matrix products, arithmetic and copies ran while one was open for 10% -> 6% of each run, Pallas kernels for 0% -> 0%
where the time goes in v1:
time: 432 us; the launch traced here: 424 us
  Pallas kernels  302 us (70%)
  matrix products  54.4 us (13%)
  other arithmetic  34.5 us (8%)
  local copies, waits for them, and re-layouts  25.1 us (6%)
  between operations  5.56 us (1%)
    pallas_call x1, Pallas kernels, reduce_grads(): pl.pallas_call(functools.partial(reduce_kernel, cplan, splan), out_shape=...  148 us
    pallas_call x1, Pallas kernels, gather_weights(): pl.pallas_call(functools.partial(gather_kernel, cplan, splan), out_shape=...  106 us
    pallas_call x1, Pallas kernels, attend_back(): pl.pallas_call(attend_back_kernel, grid=(3,), out_shape=(jax.ShapeDtypeSt...  27.2 us
    dot_general x7, matrix products, nn(): lax.dot_general(a, b, (((1,), (0,)), ((), ())), preferred_element_type=F32)  24 us
    dot_general x6, matrix products, tn(): lax.dot_general(a, b, (((0,), (0,)), ((), ())), preferred_element_type=F32)  18.7 us
    pallas_call x1, Pallas kernels, attend(): pl.pallas_call(attend_kernel, grid=(3,), out_shape=(jax.ShapeDtypeStruct(...  17.6 us
    convert_element_type x2, other arithmetic, adamw(): return (master_new, first_new, second_new, master_new.astype(BF16))  12.3 us
    dot_general x5, matrix products, nt(): lax.dot_general(a, b, (((1,), (1,)), ((), ())), preferred_element_type=F32)  9.43 us
  transfers between devices with their start and end apart: 2, of which 0 were waited for; matrix products, arithmetic and copies ran while one was open for 6% of the time, Pallas kernels for 0%

profile of v1, /device:TPU:0, one launch (start us, length us, event | category | flops | bytes accessed | tf_op | source)
XLA Modules:
  0.0 424.3 jit_solution(13788880631433713897)
XLA Ops:
  0.8 0.8 constant_dynamic-slice_fusion.2
  1.6 2.5 pad_bitcast_fusion.common_in
  4.1 6.5 %gather_fusion = bf16[160,1536]{1,0:T(8,128)(2,1)S(1)} fusion(bf16[3136,1536]{1,0:T(8,128)(2,1)} %bitcast.74, s32[1024]{0:T(1024)S(1)} %pad_clamp_fusion), kind=kCustom, calls=%fused_computation | custom fusion | bytes 983680 | tf_op jit(solution)/shard_map/jit(_take)/gather | solution.py:1456
  10.6 0.9 broadcast_select_fusion.refs_0_
  11.5 2.5 pad.32
  14.1 2.6 cosine_select_fusion.refs_1_
  16.7 0.6 stack.23.scalars
  17.3 3.5 align.1
  20.7 106.0 %gather.8 = (bf16[1536,768]{1,0:T(8,128)(2,1)}, bf16[768,384]{1,0:T(8,128)(2,1)}, bf16[384,1152]{1,0:T(8,128)(2,1)}, bf16[384,384]{1,0:T(8,128)(2,1)}, bf16[384,...) custom-call(bf16[2048,128]{1,0:T(8,128)(2,1)} %get-tuple-element.44., ...), custom_call_target="tpu_custom_call" | custom-call | tf_op jit(solution)/shard_map/gather/pallas_call | solution.py:614
  126.8 0.7 slice_bitcast_fusion
  127.5 0.9 slice_bitcast_fusion.4
  128.4 2.1 convert_reduce_fusion
  130.5 2.5 fusion.2
  133.1 0.3 iota_compare_fusion
  133.4 0.4 multiply_add_fusion
  134.0 2.3 fusion.68
  136.3 0.5 multiply_reduce_fusion
  137.0 0.5 add_convert_fusion
  137.5 0.7 copy-done.26
  138.1 1.9 convolution_convert_fusion.k_ref
  140.0 1.4 fusion.26.q_ref
  141.4 1.9 fusion.22.v_ref
  143.4 17.6 %attend.1 = (f32[784,384]{1,0:T(8,128)}, f32[3,8,784]{2,1,0:T(8,128)}) custom-call(bf16[784,384]{1,0:T(8,128)(2,1)} %fusion.26.q_ref, bf16[1568,384]{1,0:T(8,128)(2,1)} %convolution_convert_fusion.k_ref, bf16[1568,384]{1,0:T(8,128)(2,1)} %fusion.22.v_ref), custom_call_target="tpu_custom_call" | custom-call | tf_op jit(solution)/shard_map/attend/pallas_call | solution.py:1353
  161.0 2.1 fusion.69
  163.1 0.3 multiply_reduce_fusion.10
  163.4 11.6 %fusion.7 = (bf16[784,1536]{1,0:T(8,128)(2,1)S(1)}, f32[784,1536]{1,0:T(8,128)S(1)}) fusion(f32[1536]{0:T(1024)S(1)} %add.335, bf16[384,1536]{1,0:T(8,128)(2,1)S(1)} %copy-done.33, f32[784,384]{1,0:T(8,128)S(1)} %get-tuple-element.128, f32[384]{0:T(512)S(1)} %get-tuple-element.111, f32[384]{0:T(512)S(1)} %get-tuple-element.112, ...), kind=kOutput, calls=%fused_computation.12 | convolution fusion | flops 1005828096 | bytes 9624704 | tf_op jit(solution)/shard_map/dot_general | solution.py:205
  175.1 1.5 fusion.70
  176.6 0.3 multiply_reduce_fusion.9
  177.0 0.2 copy-done.22
  177.2 3.6 convert_reduce_fusion.2
  180.8 1.7 multiply_reduce_fusion.1
  182.5 0.4 copy-done
  183.0 0.5 convert_reduce_fusion.4
  183.5 3.1 convert_reduce_fusion.1
  186.6 1.7 multiply_reduce_fusion.2
  188.3 0.6 convert_reduce_fusion.5
  188.9 1.1 copy-done.3
  190.0 1.4 convolution_convert_fusion.1.do_ref
  191.5 27.2 %attend_back.1 = (bf16[784,384]{1,0:T(8,128)(2,1)}, f32[1568,384]{1,0:T(8,128)}, f32[1568,384]{1,0:T(8,128)}) custom-call(bf16[784,384]{1,0:T(8,128)(2,1)} %fusion.26.q_ref, bf16[1568,384]{1,0:T(8,128)(2,1)} %convolution_convert_fusion.k_ref, bf16[1568,384]{1,0:T(8,128)(2,1)} %fusion.22.v_ref, bf16[784,384]{1,0:T(8,128)(2,1)} %convolution_convert_fusion.1.do_ref, ...), custom_call_target="tpu_custom_call" | custom-call | tf_op jit(solution)/shard_map/attend_back/pallas_call | solution.py:1389
  218.6 2.2 dynamic-slice_convert_fusion
  220.8 2.3 collective-permute-start.1
  223.2 2.2 dynamic-slice_convert_fusion.1
  225.5 4.3 %bitcast_reduce_fusion.refs_10_ = f32[8,128]{1,0:T(8,128)} fusion(f32[784,1536]{1,0:T(8,128)} %copy-done), kind=kLoop, calls=%fused_computation.19 | loop fusion | flops 2407424 | bytes 4820992 | tf_op jit(solution)/shard_map/reduce_sum | solution.py:1495
  229.8 5.5 %fusion.62.refs_2_ = f32[384,1536]{1,0:T(8,128)} fusion(f32[784,384]{1,0:T(8,128)S(1)} %copy-done.8, f32[384]{0:T(512)S(1)} %get-tuple-element.109, f32[384]{0:T(512)S(1)} %get-tuple-element.108, f32[784]{0:T(1024)S(1)} %add_rsqrt_fusion.3, f32[784]{0:T(1024)S(1)} %broadcast_multiply_fusion.9, f32[784,1536]{1,0:T(8,128)} %copy-done), kind=kOutput, calls=%fused_computation.183 | convolution fusion | flops 928757760 | bytes 8389760 | tf_op jit(solution)/shard_map/dot_general | solution.py:209
  235.4 3.1 fusion.60.refs_3_
  238.4 1.4 fusion.35.refs_1_
  239.8 0.3 multiply_reduce_fusion.6
  240.2 0.7 constant_dynamic-slice_fusion.refs_6_
  240.9 1.3 slice.153.refs_7_
  242.3 0.6 pad.38.refs_9_
  242.9 5.3 %fusion.56.refs_4_ = f32[1536,384]{1,0:T(8,128)} fusion(bf16[784,1536]{1,0:T(8,128)(2,1)} %copy-done.35, f32[784,384]{1,0:T(8,128)} %copy-done.12), kind=kOutput, calls=%fused_computation.177 | convolution fusion | flops 925145088 | bytes 5971968 | tf_op jit(solution)/shard_map/dot_general | solution.py:209
  248.2 1.3 add_convert_fusion.1
  249.6 0.5 copy-done.17
  250.1 1.2 add_convert_fusion.2
  251.3 0.3 convert_reduce_fusion.3
  251.6 2.4 fusion.32.refs_0_
  254.0 1.5 multiply_reduce_fusion.3
  255.6 0.8 multiply_reduce_fusion.4
  256.4 1.0 convolution_convert_fusion.2.refs_5_
  257.6 0.6 select_maximum_fusion.refs_8_
  258.3 148.2 %reduce.1 = (f32[2048,128]{1,0:T(8,128)}, f32[2624,128]{1,0:T(8,128)}, f32[16,128]{1,0:T(8,128)}) custom-call(f32[384,1152]{1,0:T(8,128)} %fusion.32.refs_0_, f32[384,384]{1,0:T(8,128)} %fusion.35.refs_1_, f32[384,1536]{1,0:T(8,128)} %fusion.62.refs_2_, f32[384,1536]{1,0:T(8,128)} %fusion.60.refs_3_, f32[1536,384]{1,0:T(8,128)} %fusion.56.refs_4_, ...), custom_call_target="tpu_custom_call" | custom-call | tf_op jit(solution)/shard_map/reduce/pallas_call | solution.py:1280
  406.5 1.3 slice_reduce_fusion
  409.2 9.4 %fusion.64 = (bf16[1,258240]{1,0:T(2,128)(2,1)}, f32[1,258240]{1,0:T(1,128)}, f32[1,258240]{1,0:T(1,128)}, f32[1,258240]{1,0:T(1,128)}) fusion(f32[1,258240]{1,0:T(1,128)} %param.17, f32[]{:T(128)S(6)} %min.3, f32[1,262144]{1,0:T(1,128)} %bitcast.80, f32[1,258240]{1,0:T(1,128)} %param.18, f32[1,258240]{1,0:T(1,128)} %param.19), kind=kLoop, calls=%fused_computation.185 | loop fusion | flops 4390080 | bytes 7747204 | tf_op jit(solution)/shard_map/convert_element_type | solution.py:1543
  418.7 2.9 fusion.66
  (99 shorter events, 1.0 us)
Async XLA Ops:
  4.1 7.4 %copy-start.13 = (f32[1,258240]{1,0:T(1,128)S(1)}, f32[1,258240]{1,0:T(1,128)}, u32[]{:S(2)}) copy-start(f32[1,258240]{1,0:T(1,128)} %param.17) | copy-start | bytes 3098884
  130.5 2.9 copy-start.32
  130.5 2.9 copy-start.28
  130.5 2.9 copy-start.29
  130.5 2.9 copy-start.30
  130.5 2.9 copy-start.31
  133.1 0.9 copy-start.25
  137.0 1.2 copy-start.26
  137.5 4.0 copy-start.10
  143.4 17.6 %copy-start.23 = (bf16[384,384]{1,0:T(8,128)(2,1)S(1)}, bf16[384,384]{1,0:T(8,128)(2,1)}, u32[]{:S(2)}) copy-start(bf16[384,384]{1,0:T(8,128)(2,1)} %get-tuple-element.50) | copy-start | bytes 884740
  161.0 2.4 copy-start.33
  163.1 25.3 %copy-start.1 = (f32[784,384]{1,0:T(8,128)}, f32[784,384]{1,0:T(8,128)S(1)}, u32[]{:S(2)}) copy-start(f32[784,384]{1,0:T(8,128)S(1)} %get-tuple-element.128) | copy-start | bytes 3612676
  163.4 11.6 %copy-start.34 = (bf16[1536,384]{1,0:T(8,128)(2,1)S(1)}, bf16[1536,384]{1,0:T(8,128)(2,1)}, u32[]{:S(2)}) copy-start(bf16[1536,384]{1,0:T(8,128)(2,1)} %get-tuple-element.53) | copy-start | bytes 3538948
  175.0 1.6 copy-start.35
  175.1 2.1 copy-start.22
  176.6 6.3 %copy-start.7 = (f32[784,384]{1,0:T(8,128)}, f32[784,384]{1,0:T(8,128)S(1)}, u32[]{:S(2)}) copy-start(f32[784,384]{1,0:T(8,128)S(1)} %get-tuple-element.132) | copy-start | bytes 3612676
  180.8 2.2 copy-start
  183.5 4.9 %copy-start.12 = (f32[784,384]{1,0:T(8,128)}, f32[784,384]{1,0:T(8,128)S(1)}, u32[]{:S(2)}) copy-start(f32[784,384]{1,0:T(8,128)S(1)} %get-tuple-element.101) | copy-start | bytes 3612676
  186.6 1.7 copy-start.15
  188.9 1.1 copy-start.3
  220.8 27.4 %collective-permute-start.1 = (bf16[784,384]{1,0:T(8,128)(2,1)}, bf16[784,384]{1,0:T(8,128)(2,1)}, u32[]{:S(2)}, u32[]{:S(2)}) collective-permute-start(bf16[784,384]{1,0:T(8,128)(2,1)} %dynamic-slice_convert_fusion), channel_id=1, source_target_pairs={{0,1},{1,0},{2,3},{3,2},{4,5},{5,4},{6,7},{7,6},{8,9},{9,8},{10,11... | collective-permute-start | bytes 1806344 | tf_op jit(solution)/shard_map/ppermute | solution.py:1450
  225.3 24.3 %collective-permute-start = (bf16[784,384]{1,0:T(8,128)(2,1)}, bf16[784,384]{1,0:T(8,128)(2,1)}, u32[]{:S(2)}, u32[]{:S(2)}) collective-permute-start(bf16[784,384]{1,0:T(8,128)(2,1)} %dynamic-slice_convert_fusion.1), channel_id=1, source_target_pairs={{0,1},{1,0},{2,3},{3,2},{4,5},{5,4},{6,7},{7,6},{8,9},{9,8},{10,11... | collective-permute-start | bytes 1806344 | tf_op jit(solution)/shard_map/ppermute | solution.py:1450
  225.5 4.3 %copy-start.8 = (f32[784,384]{1,0:T(8,128)S(1)}, f32[784,384]{1,0:T(8,128)}, u32[]{:S(2)}) copy-start(f32[784,384]{1,0:T(8,128)} %copy-done.7) | copy-start | bytes 3612676
  229.8 5.5 %copy-start.2 = (f32[784,384]{1,0:T(8,128)S(1)}, f32[784,384]{1,0:T(8,128)}, u32[]{:S(2)}) copy-start(f32[784,384]{1,0:T(8,128)} %copy-done.1) | copy-start | bytes 3612676
  229.8 5.5 %copy-start.16 = (bf16[784,1536]{1,0:T(8,128)(2,1)S(1)}, bf16[784,1536]{1,0:T(8,128)(2,1)}, u32[]{:S(2)}) copy-start(bf16[784,1536]{1,0:T(8,128)(2,1)} %copy-done.15) | copy-start | bytes 7225348
  235.4 3.1 copy-start.4
  235.4 3.1 copy-start.6
  238.4 1.8 copy-start.14
  242.9 5.3 %copy-start.18 = (f32[1568,384]{1,0:T(8,128)S(1)}, f32[1568,384]{1,0:T(8,128)}, u32[]{:S(2)}) copy-start(f32[1568,384]{1,0:T(8,128)} %get-tuple-element.58) | copy-start | bytes 7225348
  248.2 1.9 copy-start.17
  249.6 1.7 copy-start.24
  249.6 2.0 copy-start.11
  251.6 2.4 copy-start.27
  254.0 1.5 copy-start.5
  409.2 9.5 %copy-start.9 = (f32[333360]{0:T(1024)S(1)}, f32[333360]{0:T(1024)}, u32[]{:S(2)}) copy-start(f32[333360]{0:T(1024)} %param.14) | copy-start | bytes 4000324
  409.2 9.5 %copy-start.19 = (f32[333360]{0:T(1024)S(1)}, f32[333360]{0:T(1024)}, u32[]{:S(2)}) copy-start(f32[333360]{0:T(1024)} %param.15) | copy-start | bytes 4000324
  409.2 9.5 %copy-start.20 = (f32[333360]{0:T(1024)S(1)}, f32[333360]{0:T(1024)}, u32[]{:S(2)}) copy-start(f32[333360]{0:T(1024)} %param.16) | copy-start | bytes 4000324
  409.2 9.5 %copy-start.21 = (f32[2624,128]{1,0:T(8,128)S(1)}, f32[2624,128]{1,0:T(8,128)}, u32[]{:S(2)}) copy-start(f32[2624,128]{1,0:T(8,128)} %get-tuple-element.76) | copy-start | bytes 4030468

commit v2 on v1

--- a/solution.py
+++ b/solution.py
@@ -213,7 +213,7 @@
 SAVED = Namespace(
     embedded=((VP, D), F32), normed_a=((VP, D), BF16), mixed=((2, VP, 576), BF16), probs=((6, VP, VP), F32), merged=((VP, 384), BF16),
     after=((VP, D), F32), normed_m=((VP, D), BF16), raised=((VP, 1536), F32), active=((VP, 1536), BF16), encoded=((VP, D), F32),
-    final_low=((VP, D), BF16), lowered=((VP, DD), F32))
+    final_low=((VP, D), BF16), lowered=((VP, DD), F32), seen=((VP, PATCH), BF16))
 NSAVED = len(vars(SAVED))
 SMALL_AT = []
 for _, _count in SMALLS:
@@ -280,8 +280,31 @@
     return jnp.concatenate([ref[at + k : at + k + 1, :] for k in range(count)], axis=1)
 
 
-def embed(pix, pos, stage, small_ref, saved):
-    saved.embedded[...] = nn(pix[...], stage.embedding[...]) + row_of(small_ref, 0, 6) + pos[...]
+def sines(width, step=32):
+    column = np.arange(width)
+    rate = 10000.0 ** (-(2 * (column // 2)) / width)
+    high, low = np.arange(0, TUBES, step)[:, None] * rate, np.arange(step)[:, None] * rate
+    even = column % 2 == 0
+    return (
+        np.where(even, np.sin(high), np.cos(high)).astype(np.float32), np.where(even, np.cos(high), -np.sin(high)).astype(np.float32),
+        np.cos(low).astype(np.float32), np.sin(low).astype(np.float32))
+
+
+def exact(a, b):
+    return lax.dot_general(a, b, (((1,), (0,)), ((), ())), precision=lax.Precision.HIGHEST, preferred_element_type=F32)
+
+
+def pick_rows(order_ref, pixel_buf, high_ref, low_ref, saved):
+    order = order_ref[...]
+    chosen = order == lax.broadcasted_iota(jnp.int32, (VP, TUBES), 1)
+    saved.seen[...] = nn(jnp.where(chosen, 1.0, 0.0).astype(BF16), pixel_buf[...]).astype(BF16)
+    high = jnp.where(lax.shift_right_logical(order, 5) == lax.broadcasted_iota(jnp.int32, (VP, 56), 1), 1.0, 0.0)
+    low = jnp.where(lax.bitwise_and(order, 31) == lax.broadcasted_iota(jnp.int32, (VP, 32), 1), 1.0, 0.0)
+    saved.embedded[...] = exact(high, high_ref[:, :D]) * exact(low, low_ref[:, :D]) + exact(high, high_ref[:, D:]) * exact(low, low_ref[:, D:])
+
+
+def embed(stage, small_ref, saved):
+    saved.embedded[...] = nn(saved.seen[...], stage.embedding[...]) + row_of(small_ref, 0, 6) + saved.embedded[...]
 
 
 def encode(stage, small_ref, bias_ref, saved, swap, while_first, while_second):
@@ -333,13 +356,15 @@
 
 
 def unpack_and_encode(cplan, splan, refs, ready):
-    pix, pos, outs, smalls, saved, (sbuf, dbuf, cbuf, wide, pair_buf), stages, out_sem, (swaps, moved, send, recv) = refs
+    (order, pixels, high, low), outs, smalls, saved, (sbuf, dbuf, cbuf, wide, pair_buf), stages, out_sem, (swaps, moved, send, recv, pixel_buf, pixel_sem) = refs
     t = lax.axis_index(TENSOR)
     y, c = t // 2, t % 2
     me = lax.axis_index(DP)
     fd = first_dec(splan)
     stage = Namespace(**dict(zip(OUT_NAMES, stages)))
     copies = []
+    pltpu.make_async_copy(pixels.at[c], pixel_buf, pixel_sem).wait()
+    pick_rows(order, pixel_buf, high, low, saved)
 
     def done(whole):
         index = [ref is whole for ref in stages].index(True)
@@ -360,7 +385,7 @@
     ready(0)
     common(CMATS[0])
     common_smalls()
-    embed(pix, pos, stage, smalls[0], saved)
+    embed(stage, smalls[0], saved)
     ready(1)
     split(0)
     split(1)
@@ -419,21 +444,21 @@
         pltpu.VMEM((5, 64, LANES), F32),
     ] + [pltpu.VMEM(vars(OUTS)[name], BF16) for name in OUT_NAMES] + [
         pltpu.SemaphoreType.DMA((len(OUT_NAMES),)), pltpu.VMEM((2, 2, VP, D), BF16), pltpu.VMEM((VP, D), BF16),
-        pltpu.SemaphoreType.DMA((3,)), pltpu.SemaphoreType.DMA((3,))]
+        pltpu.SemaphoreType.DMA((3,)), pltpu.SemaphoreType.DMA((3,)), pltpu.VMEM((TUBES, PATCH), BF16), pltpu.SemaphoreType.DMA]
 
 
 def shared_refs(refs):
     nout = len(OUT_NAMES)
-    pix, pos = refs[:2]
-    outs, smalls = refs[2 : nout + 2], refs[nout + 2 : nout + 5]
-    saved = Namespace(**dict(zip(vars(SAVED), refs[nout + 5 : nout + 5 + NSAVED])))
-    refs = refs[nout + 5 + NSAVED :]
-    return (pix, pos, outs, smalls, saved, refs[:5], refs[5 : 5 + nout], refs[5 + nout], refs[6 + nout : 10 + nout]), refs[10 + nout :]
+    outs, smalls = refs[4 : nout + 4], refs[nout + 4 : nout + 7]
+    saved = Namespace(**dict(zip(vars(SAVED), refs[nout + 7 : nout + 7 + NSAVED])))
+    rest = refs[nout + 7 + NSAVED :]
+    pltpu.make_async_copy(refs[1].at[lax.axis_index(TENSOR) % 2], rest[10 + nout], rest[11 + nout]).start()
+    return (refs[:4], outs, smalls, saved, rest[:5], rest[5 : 5 + nout], rest[5 + nout], rest[6 + nout : 12 + nout]), rest[12 + nout :]
 
 
 def gather_kernel(cplan, splan, s_own, c_own, *refs):
     shared, (send, recv, local) = shared_refs(refs)
-    sbuf, dbuf, cbuf = shared[5][:3]
+    sbuf, dbuf, cbuf = shared[4][:3]
     me, t = lax.axis_index(DP), lax.axis_index(TENSOR)
     z, x, y, c = me // 2, me % 2, t // 2, t % 2
     ty = (1 - y) * 2 + c
@@ -593,7 +618,7 @@
     barrier = pltpu.get_barrier_semaphore()
     for other in (t // 2 * 2 + 1 - t % 2, (1 - t // 2) * 2 + t % 2):
         pl.semaphore_signal(barrier, inc=1, device_id={DP: lax.axis_index(DP), TENSOR: other}, device_id_type=MESH)
-    copies = [pltpu.make_async_copy(source, target, local.at[k]) for k, (source, target) in enumerate(zip((s_all, d_all, c_all), shared[5][:3]))]
+    copies = [pltpu.make_async_copy(source, target, local.at[k]) for k, (source, target) in enumerate(zip((s_all, d_all, c_all), shared[4][:3]))]
     for copy in copies:
         copy.start()
     for copy in copies:
@@ -602,8 +627,12 @@
     unpack_and_encode(cplan, splan, shared, lambda stage: None)
 
 
-def gather_weights(common_master, split_master, pix, pos, cplan, splan):
+def gather_weights(common_master, split_master, order, pixels, cplan, splan):
     s_own, c_own = align(common_master, split_master, cplan, splan)
+    seen = lax.dynamic_index_in_dim(order, lax.axis_index(TENSOR) % 2, 0, False)[:VIS]
+    first, second, third, fourth = sines(D)
+    high = np.pad(np.concatenate([first, second], axis=1), ((0, 7), (0, 0)))
+    inputs = (jnp.pad(seen, (0, VP - VIS))[:, None], pixels, jnp.asarray(high), jnp.asarray(np.concatenate([third, fourth], axis=1)))
     any_spec = pl.BlockSpec(memory_space=pl.ANY)
     vmem = pl.BlockSpec(memory_space=pltpu.VMEM)
     scratch = unpack_scratch(cplan, splan)
@@ -613,10 +642,10 @@
     if cplan.parts == 8 and splan.parts == 8:
         results = pl.pallas_call(
             functools.partial(gather_kernel, cplan, splan),
-            out_shape=GATHERED, in_specs=[vmem] * 4, out_specs=out_specs,
+            out_shape=GATHERED, in_specs=[vmem] * 3 + [any_spec] + [vmem] * 2, out_specs=out_specs,
             scratch_shapes=scratch + [pltpu.SemaphoreType.DMA((56,)), pltpu.SemaphoreType.DMA((56,)), pltpu.SemaphoreType.DMA((2,))],
             compiler_params=params, name="gather",
-        )(s_own, c_own, pix, pos)
+        )(s_own, c_own, *inputs)
     else:
         y = lax.axis_index(TENSOR) // 2
         s_all = lax.all_gather(lax.all_gather(s_own, DP), TENSOR).reshape(2, 2, splan.parts, splan.rows, LANES)
@@ -625,9 +654,9 @@
         d_other = lax.dynamic_index_in_dim(s_all, 1 - y, 0, False)[:, fd:]
         results = pl.pallas_call(
             functools.partial(local_unpack_kernel, cplan, splan),
-            out_shape=GATHERED, in_specs=[any_spec] * 3 + [vmem] * 2, out_specs=out_specs,
+            out_shape=GATHERED, in_specs=[any_spec] * 3 + [vmem, any_spec] + [vmem] * 2, out_specs=out_specs,
             scratch_shapes=scratch + [pltpu.SemaphoreType.DMA((3,))], compiler_params=params, name="unpack",
-        )(s_mine, d_other, c_all, pix, pos)
+        )(s_mine, d_other, c_all, *inputs)
     weights = Namespace(**dict(zip(OUT_NAMES, results)))
     small, bias, dbias = results[len(OUT_NAMES) : len(OUT_NAMES) + 3]
     at = 0
@@ -753,7 +782,7 @@
 WIDE_ROWS = max(S_WIDE - SPLIT_LATE, C_WIDE - COMMON_LATE)
 BACK_WEIGHTS = OUT_NAMES[5:9] + OUT_NAMES[1:2]
 LATE_NAMES = OUT_NAMES[2:5] + OUT_NAMES[9:]
-KEPT = tuple(vars(SAVED))[:-1]
+KEPT = tuple(vars(SAVED))[:-2]
 
 
 def norm_rows_back(inputs, gain, grad):
@@ -1427,33 +1456,14 @@
     return 0.5 * (1.0 + lax.erf(inputs * math.sqrt(0.5))) + inputs * jnp.exp(-0.5 * inputs * inputs) * (1.0 / math.sqrt(2.0 * math.pi))
 
 
-def sine_rows(position, width):
-    column = jnp.arange(width)
-    exponent = (2 * (column // 2)).astype(F32) / width
-    angles = position.astype(F32)[:, None] / jnp.power(10000.0, exponent)[None, :]
-    return jnp.where((column % 2 == 0)[None, :], jnp.sin(angles), jnp.cos(angles))
-
-
 def sine_table(width, step=32):
-    column = np.arange(width)
-    rate = 10000.0 ** (-(2 * (column // 2)) / width)
-    high, low = np.arange(0, TUBES, step)[:, None] * rate, np.arange(step)[:, None] * rate
-    even = column % 2 == 0
-    a = np.where(even, np.sin(high), np.cos(high)).astype(np.float32)
-    b = np.where(even, np.cos(high), -np.sin(high)).astype(np.float32)
-    c, s = np.cos(low).astype(np.float32), np.sin(low).astype(np.float32)
-    table = a[:, None] * jnp.asarray(c)[None] + b[:, None] * jnp.asarray(s)[None]
+    first, second, third, fourth = sines(width, step)
+    table = first[:, None] * jnp.asarray(third)[None] + second[:, None] * jnp.asarray(fourth)[None]
     return table.reshape(TUBES, width)
 
 
 def beside(value):
     return lax.ppermute(value, TENSOR, [(i, i ^ 1) for i in range(4)])
-
-
-def seen_inputs(pixels, order):
-    c = lax.axis_index(TENSOR) % 2
-    seen = jnp.pad(lax.dynamic_index_in_dim(order, c, 0, False)[:VIS], (0, VP - VIS))
-    return jnp.take(pixels.reshape(2 * TUBES, PATCH), c * TUBES + seen, axis=0), sine_rows(seen, D)
 
 
 def step_grads(pixels, order, w, saved, scale_back):
@@ -1549,10 +1559,9 @@
     splan = Plan(groups, split_master.shape[1], TILE)
     masked_total = tubes.shape[0] * groups * (TUBES - VIS)
     pixel_count = masked_total * PATCH
-    seen_pixels, places = seen_inputs(tubes, tube_order)
-    w, saved = gather_weights(common_master, split_master, seen_pixels, places, cplan, splan)
+    w, saved = gather_weights(common_master, split_master, tube_order, tubes, cplan, splan)
     loss, grads, part, small, dbias = step_grads(tubes, tube_order, w, saved, 1.0 / pixel_count)
-    half = lax.dynamic_slice_in_dim(seen_pixels, lax.axis_index(TENSOR) // 2 * 768, 768, 1)
+    half = lax.dynamic_slice_in_dim(saved.seen, lax.axis_index(TENSOR) // 2 * 768, 768, 1)
     g_split, g_common, sums = reduce_grads(grads, part, half, w.enc_norms.reshape(36, LANES), small, dbias, loss, w, saved, cplan, splan)
     loss_mean = jnp.sum(sums[8:]) / pixel_count
     grad_norm = jnp.sqrt(jnp.sum(sums[:8]))

time: 432 us -> 422 us (0.977)
  local copies, waits for them, and re-layouts: 25.1 us -> 19.1 us
    gather x1 -> x0, local copies, waits for them, and re-layouts: 6.51 us -> none  [seen_inputs(): jnp.take(pixels.reshape(2 * TUBES, PATCH), c * TUBES + seen, axis=0)]
where the time goes in v2:
time: 422 us; the launch traced here: 415 us
  Pallas kernels  303 us (72%)
  matrix products  54.4 us (13%)
  other arithmetic  31 us (7%)
  local copies, waits for them, and re-layouts  19.1 us (5%)
  between operations  5.51 us (1%)
    pallas_call x1, Pallas kernels, reduce_grads(): pl.pallas_call(functools.partial(reduce_kernel, cplan, splan), out_shape=...  147 us
    pallas_call x1, Pallas kernels, gather_weights(): pl.pallas_call(functools.partial(gather_kernel, cplan, splan), out_shape=...  107 us
    pallas_call x1, Pallas kernels, attend_back(): pl.pallas_call(attend_back_kernel, grid=(3,), out_shape=(jax.ShapeDtypeSt...  27.2 us
    dot_general x7, matrix products, nn(): lax.dot_general(a, b, (((1,), (0,)), ((), ())), preferred_element_type=F32)  24 us
    dot_general x6, matrix products, tn(): lax.dot_general(a, b, (((0,), (0,)), ((), ())), preferred_element_type=F32)  18.7 us
    pallas_call x1, Pallas kernels, attend(): pl.pallas_call(attend_kernel, grid=(3,), out_shape=(jax.ShapeDtypeStruct(...  17.6 us
    convert_element_type x2, other arithmetic, adamw(): return (master_new, first_new, second_new, master_new.astype(BF16))  12.3 us
    dot_general x5, matrix products, nt(): lax.dot_general(a, b, (((1,), (1,)), ((), ())), preferred_element_type=F32)  9.43 us
  transfers between devices with their start and end apart: 2, of which 0 were waited for; matrix products, arithmetic and copies ran while one was open for 6% of the time, Pallas kernels for 0%

profile of v2, /device:TPU:0, one launch (start us, length us, event | category | flops | bytes accessed | tf_op | source)
XLA Modules:
  0.0 415.0 jit_solution(12381231479908566671)
XLA Ops:
  0.8 0.8 constant_dynamic-slice_fusion.2
  1.5 0.8 copy.25.refs_0_
  2.3 2.5 pad_bitcast_fusion.common_in
  4.8 2.5 pad.32
  7.3 0.6 stack.23.scalars
  7.9 3.5 align.1
  11.4 107.2 %gather.1 = (bf16[1536,768]{1,0:T(8,128)(2,1)}, bf16[768,384]{1,0:T(8,128)(2,1)}, bf16[384,1152]{1,0:T(8,128)(2,1)}, bf16[384,384]{1,0:T(8,128)(2,1)}, bf16[384,...) custom-call(bf16[2048,128]{1,0:T(8,128)(2,1)} %get-tuple-element.45., ...), custom_call_target="tpu_custom_call" | custom-call | tf_op jit(solution)/shard_map/gather/pallas_call | solution.py:643
  118.6 0.7 slice_bitcast_fusion
  119.3 0.9 slice_bitcast_fusion.4
  120.2 2.1 convert_reduce_fusion
  122.4 2.5 fusion.2
  124.9 0.3 iota_compare_fusion
  125.3 0.4 multiply_add_fusion
  125.7 0.2 copy-done.24
  125.9 2.3 fusion.58
  128.1 0.5 multiply_reduce_fusion
  128.8 0.5 add_convert_fusion
  129.3 0.7 copy-done.26
  130.0 1.9 convolution_convert_fusion.k_ref
  131.9 1.4 fusion.26.q_ref
  133.3 1.9 fusion.22.v_ref
  135.2 17.6 %attend.1 = (f32[784,384]{1,0:T(8,128)}, f32[3,8,784]{2,1,0:T(8,128)}) custom-call(bf16[784,384]{1,0:T(8,128)(2,1)} %fusion.26.q_ref, bf16[1568,384]{1,0:T(8,128)(2,1)} %convolution_convert_fusion.k_ref, bf16[1568,384]{1,0:T(8,128)(2,1)} %fusion.22.v_ref), custom_call_target="tpu_custom_call" | custom-call | tf_op jit(solution)/shard_map/attend/pallas_call | solution.py:1382
  152.8 2.1 fusion.59
  154.9 0.3 multiply_reduce_fusion.10
  155.3 11.6 %fusion.7 = (bf16[784,1536]{1,0:T(8,128)(2,1)S(1)}, f32[784,1536]{1,0:T(8,128)S(1)}) fusion(f32[1536]{0:T(1024)S(1)} %add.301, bf16[384,1536]{1,0:T(8,128)(2,1)S(1)} %copy-done.33, f32[784,384]{1,0:T(8,128)S(1)} %get-tuple-element.128, f32[384]{0:T(512)S(1)} %get-tuple-element.111, f32[384]{0:T(512)S(1)} %get-tuple-element.112, ...), kind=kOutput, calls=%fused_computation.11 | convolution fusion | flops 1005828096 | bytes 9624704 | tf_op jit(solution)/shard_map/dot_general | solution.py:205
  166.9 1.5 fusion.60
  168.5 0.3 multiply_reduce_fusion.9
  168.8 0.2 copy-done.21
  169.0 3.6 convert_reduce_fusion.2
  172.6 1.7 multiply_reduce_fusion.1
  174.3 0.4 copy-done
  174.8 0.5 convert_reduce_fusion.4
  175.3 3.1 convert_reduce_fusion.1
  178.4 1.7 multiply_reduce_fusion.2
  180.2 0.6 convert_reduce_fusion.5
  180.8 1.0 copy-done.3
  181.8 1.4 convolution_convert_fusion.1.do_ref
  183.2 27.2 %attend_back.1 = (bf16[784,384]{1,0:T(8,128)(2,1)}, f32[1568,384]{1,0:T(8,128)}, f32[1568,384]{1,0:T(8,128)}) custom-call(bf16[784,384]{1,0:T(8,128)(2,1)} %fusion.26.q_ref, bf16[1568,384]{1,0:T(8,128)(2,1)} %convolution_convert_fusion.k_ref, bf16[1568,384]{1,0:T(8,128)(2,1)} %fusion.22.v_ref, bf16[784,384]{1,0:T(8,128)(2,1)} %convolution_convert_fusion.1.do_ref, ...), custom_call_target="tpu_custom_call" | custom-call | tf_op jit(solution)/shard_map/attend_back/pallas_call | solution.py:1418
  210.4 2.2 dynamic-slice_convert_fusion
  212.5 2.4 collective-permute-start.1
  214.9 2.2 dynamic-slice_convert_fusion.1
  217.3 4.3 %bitcast_reduce_fusion.refs_10_ = f32[8,128]{1,0:T(8,128)} fusion(f32[784,1536]{1,0:T(8,128)} %copy-done), kind=kLoop, calls=%fused_computation.18 | loop fusion | flops 2407424 | bytes 4820992 | tf_op jit(solution)/shard_map/reduce_sum | solution.py:1505
  221.6 5.5 %fusion.52.refs_2_ = f32[384,1536]{1,0:T(8,128)} fusion(f32[784,384]{1,0:T(8,128)S(1)} %copy-done.8, f32[384]{0:T(512)S(1)} %get-tuple-element.109, f32[384]{0:T(512)S(1)} %get-tuple-element.108, f32[784]{0:T(1024)S(1)} %add_rsqrt_fusion.3, f32[784]{0:T(1024)S(1)} %broadcast_multiply_fusion.9, f32[784,1536]{1,0:T(8,128)} %copy-done), kind=kOutput, calls=%fused_computation.161 | convolution fusion | flops 928757760 | bytes 8389760 | tf_op jit(solution)/shard_map/dot_general | solution.py:209
  227.1 3.1 fusion.50.refs_3_
  230.2 1.4 fusion.35.refs_1_
  231.6 0.3 multiply_reduce_fusion.6
  231.9 0.7 constant_dynamic-slice_fusion.refs_6_
  232.6 1.3 slice.153.refs_7_
  234.0 0.6 pad.38.refs_9_
  234.6 5.3 %fusion.46.refs_4_ = f32[1536,384]{1,0:T(8,128)} fusion(bf16[784,1536]{1,0:T(8,128)(2,1)} %copy-done.35, f32[784,384]{1,0:T(8,128)} %copy-done.12), kind=kOutput, calls=%fused_computation.155 | convolution fusion | flops 925145088 | bytes 5971968 | tf_op jit(solution)/shard_map/dot_general | solution.py:209
  239.9 1.3 add_convert_fusion.1
  241.3 0.5 copy-done.16
  241.8 1.2 add_convert_fusion.2
  243.0 0.3 convert_reduce_fusion.3
  243.4 2.4 fusion.32.refs_0_
  245.8 1.5 multiply_reduce_fusion.3
  247.3 0.8 multiply_reduce_fusion.4
  248.1 1.0 convolution_convert_fusion.2.refs_5_
  249.2 0.2 concatenate.42
  249.4 0.6 select_maximum_fusion.refs_8_
  250.0 147.2 %reduce.1 = (f32[2048,128]{1,0:T(8,128)}, f32[2624,128]{1,0:T(8,128)}, f32[16,128]{1,0:T(8,128)}) custom-call(f32[384,1152]{1,0:T(8,128)} %fusion.32.refs_0_, f32[384,384]{1,0:T(8,128)} %fusion.35.refs_1_, f32[384,1536]{1,0:T(8,128)} %fusion.52.refs_2_, f32[384,1536]{1,0:T(8,128)} %fusion.50.refs_3_, f32[1536,384]{1,0:T(8,128)} %fusion.46.refs_4_, ...), custom_call_target="tpu_custom_call" | custom-call | tf_op jit(solution)/shard_map/reduce/pallas_call | solution.py:1309
  397.2 1.3 slice_reduce_fusion
  399.9 9.4 %fusion.54 = (bf16[1,258240]{1,0:T(2,128)(2,1)}, f32[1,258240]{1,0:T(1,128)}, f32[1,258240]{1,0:T(1,128)}, f32[1,258240]{1,0:T(1,128)}) fusion(f32[1,258240]{1,0:T(1,128)} %param.19, f32[]{:T(128)S(6)} %min.3, f32[1,262144]{1,0:T(1,128)} %bitcast.80, f32[1,258240]{1,0:T(1,128)} %param.20, f32[1,258240]{1,0:T(1,128)} %param.21), kind=kLoop, calls=%fused_computation.163 | loop fusion | flops 4390080 | bytes 7747204 | tf_op jit(solution)/shard_map/convert_element_type | solution.py:1553
  409.4 2.9 fusion.56
  (93 shorter events, 0.6 us)
Async XLA Ops:
  0.6 4.1 copy-start.13
  122.3 2.9 copy-start.32
  122.3 2.9 copy-start.28
  122.3 2.9 copy-start.29
  122.4 2.9 copy-start.30
  122.4 2.9 copy-start.31
  124.9 0.9 copy-start.24
  128.8 1.2 copy-start.26
  129.3 4.0 copy-start.10
  135.2 17.6 %copy-start.22 = (bf16[384,384]{1,0:T(8,128)(2,1)S(1)}, bf16[384,384]{1,0:T(8,128)(2,1)}, u32[]{:S(2)}) copy-start(bf16[384,384]{1,0:T(8,128)(2,1)} %get-tuple-element.51) | copy-start | bytes 884740
  152.8 2.4 copy-start.33
  154.9 25.3 %copy-start.1 = (f32[784,384]{1,0:T(8,128)}, f32[784,384]{1,0:T(8,128)S(1)}, u32[]{:S(2)}) copy-start(f32[784,384]{1,0:T(8,128)S(1)} %get-tuple-element.128) | copy-start | bytes 3612676
  155.3 11.6 %copy-start.34 = (bf16[1536,384]{1,0:T(8,128)(2,1)S(1)}, bf16[1536,384]{1,0:T(8,128)(2,1)}, u32[]{:S(2)}) copy-start(bf16[1536,384]{1,0:T(8,128)(2,1)} %get-tuple-element.54) | copy-start | bytes 3538948
  166.9 1.6 copy-start.35
  166.9 2.1 copy-start.21
  168.4 6.3 %copy-start.7 = (f32[784,384]{1,0:T(8,128)}, f32[784,384]{1,0:T(8,128)S(1)}, u32[]{:S(2)}) copy-start(f32[784,384]{1,0:T(8,128)S(1)} %get-tuple-element.132) | copy-start | bytes 3612676
  172.6 2.2 copy-start
  175.3 4.9 %copy-start.12 = (f32[784,384]{1,0:T(8,128)}, f32[784,384]{1,0:T(8,128)S(1)}, u32[]{:S(2)}) copy-start(f32[784,384]{1,0:T(8,128)S(1)} %get-tuple-element.103) | copy-start | bytes 3612676
  178.4 1.7 copy-start.14
  180.7 1.0 copy-start.3
  212.5 27.4 %collective-permute-start.1 = (bf16[784,384]{1,0:T(8,128)(2,1)}, bf16[784,384]{1,0:T(8,128)(2,1)}, u32[]{:S(2)}, u32[]{:S(2)}) collective-permute-start(bf16[784,384]{1,0:T(8,128)(2,1)} %dynamic-slice_convert_fusion), channel_id=1, source_target_pairs={{0,1},{1,0},{2,3},{3,2},{4,5},{5,4},{6,7},{7,6},{8,9},{9,8},{10,11... | collective-permute-start | bytes 1806344 | tf_op jit(solution)/shard_map/ppermute | solution.py:1466
  217.0 24.3 %collective-permute-start = (bf16[784,384]{1,0:T(8,128)(2,1)}, bf16[784,384]{1,0:T(8,128)(2,1)}, u32[]{:S(2)}, u32[]{:S(2)}) collective-permute-start(bf16[784,384]{1,0:T(8,128)(2,1)} %dynamic-slice_convert_fusion.1), channel_id=1, source_target_pairs={{0,1},{1,0},{2,3},{3,2},{4,5},{5,4},{6,7},{7,6},{8,9},{9,8},{10,11... | collective-permute-start | bytes 1806344 | tf_op jit(solution)/shard_map/ppermute | solution.py:1466
  217.3 4.3 %copy-start.8 = (f32[784,384]{1,0:T(8,128)S(1)}, f32[784,384]{1,0:T(8,128)}, u32[]{:S(2)}) copy-start(f32[784,384]{1,0:T(8,128)} %copy-done.7) | copy-start | bytes 3612676
  221.6 5.5 %copy-start.2 = (f32[784,384]{1,0:T(8,128)S(1)}, f32[784,384]{1,0:T(8,128)}, u32[]{:S(2)}) copy-start(f32[784,384]{1,0:T(8,128)} %copy-done.1) | copy-start | bytes 3612676
  221.6 5.5 %copy-start.15 = (bf16[784,1536]{1,0:T(8,128)(2,1)S(1)}, bf16[784,1536]{1,0:T(8,128)(2,1)}, u32[]{:S(2)}) copy-start(bf16[784,1536]{1,0:T(8,128)(2,1)} %copy-done.14) | copy-start | bytes 7225348
  227.1 3.1 copy-start.4
  227.1 3.1 copy-start.6
  230.2 1.7 copy-start.25
  234.6 5.3 %copy-start.17 = (f32[1568,384]{1,0:T(8,128)S(1)}, f32[1568,384]{1,0:T(8,128)}, u32[]{:S(2)}) copy-start(f32[1568,384]{1,0:T(8,128)} %get-tuple-element.59) | copy-start | bytes 7225348
  239.9 1.9 copy-start.16
  241.3 1.7 copy-start.23
  241.3 2.0 copy-start.11
  243.4 2.4 copy-start.27
  245.8 1.5 copy-start.5
  399.9 9.5 %copy-start.9 = (f32[333360]{0:T(1024)S(1)}, f32[333360]{0:T(1024)}, u32[]{:S(2)}) copy-start(f32[333360]{0:T(1024)} %param.16) | copy-start | bytes 4000324
  399.9 9.5 %copy-start.18 = (f32[333360]{0:T(1024)S(1)}, f32[333360]{0:T(1024)}, u32[]{:S(2)}) copy-start(f32[333360]{0:T(1024)} %param.17) | copy-start | bytes 4000324
  399.9 9.5 %copy-start.19 = (f32[333360]{0:T(1024)S(1)}, f32[333360]{0:T(1024)}, u32[]{:S(2)}) copy-start(f32[333360]{0:T(1024)} %param.18) | copy-start | bytes 4000324
  399.9 9.5 %copy-start.20 = (f32[2624,128]{1,0:T(8,128)S(1)}, f32[2624,128]{1,0:T(8,128)}, u32[]{:S(2)}) copy-start(f32[2624,128]{1,0:T(8,128)} %get-tuple-element.78) | copy-start | bytes 4030468
